TPU v7x, 256 devices: a whole 4x4x8 slice. The times are simulated.
256 devices in a mesh: seq: 32 (over x, z_lo, core), head: 8 (over y, z_hi).
Axes of the slice: x: 4, y: 4, z: 8 (z_hi: 2, z_lo: 4; z = z_hi * 4 + z_lo), core: 2. Of those that a mesh axis runs over, the one named last changes fastest.
Arguments:
- tokens: bfloat16 [16384, 1024], P('seq'), may hold values from -6 to 6
- mem_query_w: bfloat16 [1024, 1024], P(None, 'head'), may hold values from -0.1875 to 0.1875
- mem_key_w: bfloat16 [1024, 1024], P(None, 'head'), may hold values from -0.1875 to 0.1875
- mem_value_w: bfloat16 [1024, 1024], P(None, 'head'), may hold values from -0.1875 to 0.1875
- mem_in: float32 [1024, 1024], P(None, 'head'), may hold values from -0.1875 to 0.1875
- mem_out: float32 [1024, 1024], P('head'), may hold values from -0.1875 to 0.1875
- forget_levels: float32 [16, 1024], P(None, 'head'), may hold values from 0.003 to 0.3
- momentum_levels: float32 [16, 1024], P(None, 'head'), may hold values from 0.2 to 0.9
- step_levels: float32 [16, 1024], P(None, 'head'), may hold values from 0.02 to 0.2
- plan: int32 [32], P('seq'), may hold values from 0 to 15
- norm_gain: float32 [1024], replicated, may hold values from 0.5 to 1.5
- attn_query_w: bfloat16 [1024, 1024], P(None, 'head'), may hold values from -1 to 1
- attn_key_w: bfloat16 [1024, 1024], P(None, 'head'), may hold values from -4 to 4
- attn_value_w: bfloat16 [1024, 1024], P(None, 'head'), may hold values from -0.1875 to 0.1875
- attn_out_w: bfloat16 [1024, 1024], P('head'), may hold values from -0.25 to 0.25
Outputs:
- layer_out: bfloat16 [16384, 1024], P('seq', 'head')
All inputs are finite; a program needn't handle non-finite values.
Results may differ from a plain program's by a relative error of at most 0.014.
Values may be sent and summed in bfloat16 or wider, within the bound.
A program may use at most 128 MiB of HBM per device.

v0:
```python
import jax
import jax.numpy as jnp
from jax import lax
from jax.sharding import Mesh
from jax.sharding import PartitionSpec as P

HEAD_DIM = 64
SPAN = 8
SEQ = ("seq_0", "seq_1", "seq_2")


epsilon = 1e-06


def split_up(value, dim, length):
    before, after = (value.shape[:dim], value.shape[dim + 1 :])
    return jnp.moveaxis(value.reshape(*before, length, -1, *after), dim, 0)


def sent_and_summed(value, axis, dim):
    length = lax.axis_size(axis)
    blocks = lax.all_to_all(split_up(value, dim, length), axis, 0, 0, tiled=True)
    return jnp.sum(blocks, axis=0)


def filled_with(value, identity):
    return jax.tree.map(
        lambda a, e: jnp.broadcast_to(jnp.asarray(e, a.dtype), a.shape), value, identity
    )


def gathered_once(value, axis):
    leaves = jax.tree.leaves(value)
    sequence = sorted(range(len(leaves)), key=lambda k: -leaves[k].size)
    width = (1, *leaves[sequence[0]].shape)[-1]
    lines = [
        jnp.pad(leaves[k].reshape(-1), (0, -leaves[k].size % width)).reshape(-1, width)
        for k in sequence
    ]
    both, at, found = (lax.all_gather(jnp.concatenate(lines), axis), 0, {})
    for k, line in zip(sequence, lines):
        section = both[:, at : at + len(line)].reshape(len(both), -1)
        found[k] = section[:, : leaves[k].size].reshape(-1, *leaves[k].shape)
        at += len(line)
    numbers = iter(range(len(leaves)))
    return jax.tree.map(lambda _: found[next(numbers)], value)


def carried_in(value, axes, combine, identity):
    before = start = filled_with(value, identity)
    running = value
    for axis in reversed(axes):
        length, index = (lax.axis_size(axis), lax.axis_index(axis))
        pieces = gathered_once(running, axis)
        inside, running = (start, start)
        for k in range(length):
            passed = k < index
            running = combine(running, jax.tree.map(lambda part: part[k], pieces))
            inside = jax.tree.map(lambda new, old: jnp.where(passed, new, old), running, inside)
        before = combine(inside, before)
    return before


def shifted(value, axis, by):
    length = lax.axis_size(axis)
    pairs = [(i, i + by) for i in range(length) if 0 <= i + by < length]
    return lax.ppermute(value, axis, pairs)


def sum_at_owner(value, axis, dim):
    length = lax.axis_size(axis)
    blocks = lax.all_to_all(split_up(value, dim, length), axis, 0, 0, tiled=True)
    return jnp.sum(blocks.astype(jnp.float32), axis=0)


def silu_slope(values):
    sigmoid = jax.nn.sigmoid(values)
    return sigmoid * (1.0 + values * (1.0 - sigmoid))


def project(left, weight):
    return jnp.dot(left, weight, preferred_element_type=jnp.float32).astype(jnp.bfloat16)


def normalize(retrieved, norm_gain):
    mean_square = jnp.mean(retrieved * retrieved, axis=-1, keepdims=True)
    return (retrieved * lax.rsqrt(mean_square + epsilon) * norm_gain).astype(jnp.bfloat16)


def lookup(table, chosen):
    matches = jnp.arange(table.shape[0], dtype=jnp.int32)[:, None] == chosen
    return jnp.sum(jnp.where(matches, table, 0.0), axis=0)


def as_columns(vector):
    return vector[..., None, :]


def as_rows(vector):
    return vector[..., :, None]


def compose(earlier, later):
    (
        prior_decay,
        prior_cross,
        prior_keep,
        prior_speed_in,
        prior_speed_out,
        prior_weight_in,
        prior_weight_out,
    ) = earlier
    (
        after_decay,
        after_cross,
        after_keep,
        after_speed_in,
        after_speed_out,
        after_weight_in,
        after_weight_out,
    ) = later
    decay = after_decay * prior_decay
    cross = after_cross * prior_decay + after_keep * prior_cross
    keep = after_keep * prior_keep
    speed_in = as_columns(after_decay) * prior_speed_in + after_speed_in
    speed_out = as_rows(after_decay) * prior_speed_out + after_speed_out
    weight_in = (
        as_columns(after_cross) * prior_speed_in
        + as_columns(after_keep) * prior_weight_in
        + after_weight_in
    )
    weight_out = (
        as_rows(after_cross) * prior_speed_out
        + as_rows(after_keep) * prior_weight_out
        + after_weight_out
    )
    return (decay, cross, keep, speed_in, speed_out, weight_in, weight_out)


def window_attend(query, keys, values, block_index):
    query_count = query.shape[0]
    key_count = keys.shape[0]
    span_rows = key_count - query_count
    distance = (
        span_rows
        + jnp.arange(query_count, dtype=jnp.int32)[:, None]
        - jnp.arange(key_count, dtype=jnp.int32)[None, :]
    )
    key_pos = (block_index * query_count - span_rows + jnp.arange(key_count, dtype=jnp.int32))[
        None, :
    ]
    allowed = (distance >= 0) & (distance < span_rows) & (key_pos >= 0)
    contexts = []
    for head_number in range(query.shape[1] // HEAD_DIM):
        low_col = head_number * HEAD_DIM
        scores = jnp.einsum(
            "qd,kd->qk",
            query[:, low_col : low_col + HEAD_DIM],
            keys[:, low_col : low_col + HEAD_DIM],
            preferred_element_type=jnp.float32,
        ) * HEAD_DIM ** (-0.5)
        scores = jnp.where(allowed, scores, -1e30)
        row_peak = jnp.max(scores, axis=-1, keepdims=True)
        weights = jnp.exp(scores - row_peak)
        probabilities = (weights / jnp.sum(weights, axis=-1, keepdims=True)).astype(jnp.bfloat16)
        contexts.append(
            jnp.dot(
                probabilities,
                values[:, low_col : low_col + HEAD_DIM],
                preferred_element_type=jnp.float32,
            ).astype(jnp.bfloat16)
        )
    return jnp.concatenate(contexts, axis=1)


def shards(
    tokens,
    mem_query_w,
    mem_key_w,
    mem_value_w,
    mem_in,
    mem_out,
    forget_levels,
    momentum_levels,
    step_levels,
    plan,
    norm_gain,
    attn_query_w,
    attn_key_w,
    attn_value_w,
    attn_out_w,
):
    tok_rows = tokens.shape[0]
    share_rows = tok_rows // lax.axis_size("head")
    my_start = lax.axis_index("head") * share_rows
    mem_query, mem_key, mem_value = (
        lax.all_gather(project(tokens, mem_query_w), "head", axis=1, tiled=True),
        lax.all_gather(project(tokens, mem_key_w), "head", axis=1, tiled=True),
        lax.all_gather(project(tokens, mem_value_w), "head", axis=1, tiled=True),
    )
    keys_wide = mem_key.astype(jnp.float32)
    pre_act = jnp.dot(keys_wide, mem_in)
    hidden = jax.nn.silu(pre_act)
    predicted = sent_and_summed(jnp.dot(hidden, mem_out), "head", 0)
    value_share = lax.dynamic_slice_in_dim(mem_value, my_start, share_rows, 0).astype(jnp.float32)
    residual_err = lax.all_gather(
        2.0 / tok_rows * (predicted - value_share), "head", axis=0, tiled=True
    )
    grad_out = jnp.dot(hidden.T, residual_err)
    slope_term = jnp.dot(residual_err, mem_out.T) * silu_slope(pre_act)
    grad_in = jnp.dot(keys_wide.T, slope_term)
    chosen = plan[0]
    forget = lookup(forget_levels, chosen)
    momentum = lookup(momentum_levels, chosen)
    step_rate = lookup(step_levels, chosen)
    change_in = -as_columns(step_rate) * grad_in
    change_out = -as_rows(step_rate) * grad_out
    element = (momentum, momentum, 1.0 - forget, change_in, change_out, change_in, change_out)
    identity = (
        jnp.ones_like(momentum),
        jnp.zeros_like(momentum),
        jnp.ones_like(momentum),
        jnp.zeros_like(grad_in),
        jnp.zeros_like(grad_out),
        jnp.zeros_like(grad_in),
        jnp.zeros_like(grad_out),
    )
    entering = carried_in(element, SEQ, compose, identity)
    weight_in = as_columns(entering[2]) * mem_in + entering[5]
    weight_out = as_rows(entering[2]) * mem_out + entering[6]
    query_hidden = jax.nn.silu(jnp.dot(mem_query.astype(jnp.float32), weight_in))
    retrieved = sent_and_summed(jnp.dot(query_hidden, weight_out), "head", 0)
    normed = lax.all_gather(normalize(retrieved, norm_gain), "head", axis=0, tiled=True)
    att_query = project(normed, attn_query_w)
    att_key = project(normed, attn_key_w)
    att_value = project(normed, attn_value_w)
    earlier = []
    for distance in range(SPAN, 0, -1):
        earlier.append(shifted((att_key, att_value), SEQ, distance))
    key_window = jnp.concatenate([received[0] for received in earlier] + [att_key], axis=0)
    value_window = jnp.concatenate([received[1] for received in earlier] + [att_value], axis=0)
    context = window_attend(att_query, key_window, value_window, lax.axis_index(SEQ))
    partial_out = jnp.dot(context, attn_out_w, preferred_element_type=jnp.float32)
    return sum_at_owner(partial_out.astype(jnp.bfloat16), "head", 1).astype(jnp.bfloat16)


def solution(mesh):
    split = Mesh(
        mesh.devices.reshape(4, 4, 2, mesh.shape["head"]), ("seq_0", "seq_1", "seq_2", "head")
    )
    in_specs = (
        P(SEQ, None),
        P(None, "head"),
        P(None, "head"),
        P(None, "head"),
        P(None, "head"),
        P("head", None),
        P(None, "head"),
        P(None, "head"),
        P(None, "head"),
        P(SEQ),
        P(),
        P(None, "head"),
        P(None, "head"),
        P(None, "head"),
        P("head", None),
    )
    out_specs = P(SEQ, "head")
    return jax.shard_map(
        shards, mesh=split, in_specs=in_specs, out_specs=out_specs, check_vma=False
    )
```

profile of v0, /device:TPU:6, one launch (start us, length us, event | category | flops | bytes accessed | tf_op | source)
XLA Modules:
  0.0 805.0 jit_solution(12139986413345933075)
XLA Ops:
  9.8 64.6 %all-gather.17.cloned.1.call-done = bf16[512,1024]{1,0:T(8,128)(2,1)} async-done(((bf16[512,128]{1,0:T(8,128)(2,1)}), bf16[512,1024]{1,0:T(8,128)(2,1)}) %all-gather.17.cloned.1.call-update) | async-done | bytes 1048592 | tf_op jit(solution)/shard_map/all_gather | solution.py:198
  78.7 3.8 all-to-all-start
  83.8 25.1 %all-to-all-done = f32[8,64,1024]{2,1,0:T(8,128)S(1)} async-done(((f32[8,64,1024]{2,1,0:T(8,128)}), f32[8,64,1024]{2,1,0:T(8,128)S(1)}, u32[]{:S(2)}, u32[]{:S(2)}) %all-to-all-start) | async-done | bytes 2097184 | tf_op jit(solution)/shard_map/all_to_all | solution.py:22
  109.0 51.9 %all-gather.19.cloned.1.call-done = bf16[512,1024]{1,0:T(8,128)(2,1)} async-done(((bf16[512,128]{1,0:T(8,128)(2,1)}), bf16[512,1024]{1,0:T(8,128)(2,1)}) %all-gather.19.cloned.1.call-update) | async-done | bytes 1048592 | tf_op jit(solution)/shard_map/all_gather | solution.py:199
  163.4 57.5 %all-gather.21.cloned.1.call-done = bf16[512,1024]{1,0:T(8,128)(2,1)} async-done(((bf16[64,1024]{1,0:T(8,128)(2,1)}), bf16[512,1024]{1,0:T(8,128)(2,1)}) %all-gather.21.cloned.1.call-update) | async-done | bytes 1048592 | tf_op jit(solution)/shard_map/all_gather | solution.py:206
  225.4 4.1 concatenate.18
  229.5 14.7 %all-gather.25.cloned.1.call-done = f32[2,4099,128]{2,1,0:T(8,128)} async-done(((f32[1,4099,128]{2,1,0:T(8,128)}), f32[2,4099,128]{2,1,0:T(8,128)}) %all-gather.25.cloned.1.call-update) | async-done | bytes 4197392 | tf_op jit(solution)/shard_map/all_gather | solution.py:40
  251.3 4.1 concatenate.19
  255.5 154.8 %all-gather.27.cloned.1.call-done = f32[4,4099,128]{2,1,0:T(8,128)} async-done(((f32[1,4099,128]{2,1,0:T(8,128)}), f32[4,4099,128]{2,1,0:T(8,128)}) %all-gather.27.cloned.1.call-update) | async-done | bytes 8394768 | tf_op jit(solution)/shard_map/all_gather | solution.py:40
  419.3 4.0 bitcast_add_fusion
  423.4 4.1 concatenate.20
  434.3 3.4 fusion.353
  447.0 64.8 %all-gather.29.cloned.1.call-done = f32[4,4099,128]{2,1,0:T(8,128)} async-done(((f32[1,4099,128]{2,1,0:T(8,128)}), f32[4,4099,128]{2,1,0:T(8,128)}) %all-gather.29.cloned.1.call-update) | async-done | bytes 8394768 | tf_op jit(solution)/shard_map/all_gather | solution.py:40
  511.8 3.4 fusion.352
  526.1 51.9 %all-gather.15.cloned.1.call-done = bf16[512,1024]{1,0:T(8,128)(2,1)} async-done(((bf16[512,128]{1,0:T(8,128)(2,1)}), bf16[512,1024]{1,0:T(8,128)(2,1)}) %all-gather.15.cloned.1.call-update) | async-done | bytes 1048592 | tf_op jit(solution)/shard_map/all_gather | solution.py:197
  578.0 11.3 %fusion.57 = f32[512,1024]{1,0:T(8,128)} fusion(f32[128,1024]{1,0:T(8,128)} %squeeze.275, f32[128,1024]{1,0:T(8,128)} %squeeze.274, f32[128,1024]{1,0:T(8,128)} %squeeze.273, f32[128,1024]{1,0:T(8,128)} %squeeze.272, f32[128,1024]{1,0:T(8,128)} %squeeze.271, f32[128,1024]{1,0:T(8,128)} %squeeze.270, f32[128,1024]{1,0:T(8,128)} %squeeze.269, ...), kind=kOutput, calls=%fused_computation.101 | convolution fusion | flops 287834112 | bytes 25205248 | tf_op jit(solution)/shard_map/dot_general | solution.py:232
  589.3 29.9 %all_to_all.15 = f32[8,64,1024]{2,1,0:T(8,128)S(1)} all-to-all(f32[8,64,1024]{2,1,0:T(8,128)} %bitcast.561), channel_id=1, replica_groups=mesh['seq_0'=4,'seq_1'=4,'seq_2'=2,'head'=8] {'head'}, dimensions={0} | all-to-all | bytes 4194304 | tf_op jit(solution)/shard_map/all_to_all | solution.py:22
  620.8 80.5 %all-gather.23.cloned.1.call-done = bf16[512,1024]{1,0:T(8,128)(2,1)} async-done(((bf16[64,1024]{1,0:T(8,128)(2,1)}), bf16[512,1024]{1,0:T(8,128)(2,1)}) %all-gather.23.cloned.1.call-update) | async-done | bytes 1048592 | tf_op jit(solution)/shard_map/all_gather | solution.py:233
  717.0 7.4 collective-permute-start.6
  727.8 3.0 collective-permute-done.4
  738.8 4.3 fusion.356
  743.1 4.2 fusion.355
  753.5 3.9 collective-permute-done.13
  767.9 29.4 %all_to_all.16 = bf16[8,512,128]{2,1,0:T(8,128)(2,1)S(1)} all-to-all(bf16[8,512,128]{2,1,0:T(8,128)(2,1)S(1)} %bitcast.560), channel_id=1, replica_groups=mesh['seq_0'=4,'seq_1'=4,'seq_2'=2,'head'=8] {'head'}, dimensions={0} | all-to-all | bytes 2097152 | tf_op jit(solution)/shard_map/all_to_all | solution.py:72
  (210 shorter events, 103.6 us)
Async XLA Ops:
  6.5 67.9 %all-gather.17.cloned.1.call-start = ((), (), s32[]{:S(2)}) async-start(), calls=%async_computation.4 | async-start | bytes 1179648 | tf_op jit(solution)/shard_map/all_gather | solution.py:198
  78.7 30.2 %all-to-all-start = ((f32[8,64,1024]{2,1,0:T(8,128)}), f32[8,64,1024]{2,1,0:T(8,128)S(1)}, u32[]{:S(2)}, u32[]{:S(2)}) async-start(f32[8,64,1024]{2,1,0:T(8,128)} %bitcast.559), calls=%async_computation | async-start | bytes 4194304 | tf_op jit(solution)/shard_map/all_to_all | solution.py:22
  82.5 78.4 %all-gather.19.cloned.1.call-start = ((), (), s32[]{:S(2)}) async-start(), calls=%async_computation.5 | async-start | bytes 1179648 | tf_op jit(solution)/shard_map/all_gather | solution.py:199
  83.7 137.2 %all-gather.21.cloned.1.call-start = ((), (), s32[]{:S(2)}) async-start(), calls=%async_computation.6 | async-start | bytes 1179648 | tf_op jit(solution)/shard_map/all_gather | solution.py:206
  162.5 81.7 %all-gather.25.cloned.1.call-start = ((), (), s32[]{:S(2)}) async-start(), calls=%async_computation.8 | async-start | bytes 6303744 | tf_op jit(solution)/shard_map/all_gather | solution.py:40
  229.5 180.8 %all-gather.27.cloned.1.call-start = ((), (), s32[]{:S(2)}) async-start(), calls=%async_computation.9 | async-start | bytes 10506240 | tf_op jit(solution)/shard_map/all_gather | solution.py:40
  255.4 256.4 %all-gather.29.cloned.1.call-start = ((), (), s32[]{:S(2)}) async-start(), calls=%async_computation.10 | async-start | bytes 10506240 | tf_op jit(solution)/shard_map/all_gather | solution.py:40
  427.5 150.5 %all-gather.15.cloned.1.call-start = ((), (), s32[]{:S(2)}) async-start(), calls=%async_computation.3 | async-start | bytes 1179648 | tf_op jit(solution)/shard_map/all_gather | solution.py:197
  428.7 272.6 %all-gather.23.cloned.1.call-start = ((), (), s32[]{:S(2)}) async-start(), calls=%async_computation.7 | async-start | bytes 1179648 | tf_op jit(solution)/shard_map/all_gather | solution.py:233
  703.0 11.2 %collective-permute-start = (bf16[512,128]{1,0:T(8,128)(2,1)S(1)}, bf16[512,128]{1,0:T(8,128)(2,1)S(1)}, u32[]{:S(2)}, u32[]{:S(2)}) collective-permute-start(bf16[512,128]{1,0:T(8,128)(2,1)S(1)} %convolution_convert_fusion.2), channel_id=1, source_target_pairs={{0,64},{8,72},{16,80},{24,88},{32,96},{40,104},{48,112},{56,120},{... | collective-permute-start | bytes 393224 | tf_op jit(solution)/shard_map/ppermute | solution.py:67
  704.3 12.7 %collective-permute-start.1 = (bf16[512,128]{1,0:T(8,128)(2,1)S(1)}, bf16[512,128]{1,0:T(8,128)(2,1)S(1)}, u32[]{:S(2)}, u32[]{:S(2)}) collective-permute-start(bf16[512,128]{1,0:T(8,128)(2,1)S(1)} %convolution_convert_fusion.2), channel_id=1, source_target_pairs={{0,56},{8,64},{16,72},{24,80},{32,88},{40,96},{48,104},{56,112},{6... | collective-permute-start | bytes 393224 | tf_op jit(solution)/shard_map/ppermute | solution.py:67
  706.3 18.2 %collective-permute-start.2 = (bf16[512,128]{1,0:T(8,128)(2,1)S(1)}, bf16[512,128]{1,0:T(8,128)(2,1)S(1)}, u32[]{:S(2)}, u32[]{:S(2)}) collective-permute-start(bf16[512,128]{1,0:T(8,128)(2,1)S(1)} %convolution_convert_fusion.2), channel_id=1, source_target_pairs={{0,48},{8,56},{16,64},{24,72},{32,80},{40,88},{48,96},{56,104},{64... | collective-permute-start | bytes 393224 | tf_op jit(solution)/shard_map/ppermute | solution.py:67
  708.2 18.2 %collective-permute-start.3 = (bf16[512,128]{1,0:T(8,128)(2,1)S(1)}, bf16[512,128]{1,0:T(8,128)(2,1)S(1)}, u32[]{:S(2)}, u32[]{:S(2)}) collective-permute-start(bf16[512,128]{1,0:T(8,128)(2,1)S(1)} %convolution_convert_fusion.2), channel_id=1, source_target_pairs={{0,40},{8,48},{16,56},{24,64},{32,72},{40,80},{48,88},{56,96},{64,... | collective-permute-start | bytes 393224 | tf_op jit(solution)/shard_map/ppermute | solution.py:67
  710.1 20.6 %collective-permute-start.4 = (bf16[512,128]{1,0:T(8,128)(2,1)S(1)}, bf16[512,128]{1,0:T(8,128)(2,1)S(1)}, u32[]{:S(2)}, u32[]{:S(2)}) collective-permute-start(bf16[512,128]{1,0:T(8,128)(2,1)S(1)} %convolution_convert_fusion.2), channel_id=1, source_target_pairs={{0,32},{8,40},{16,48},{24,56},{32,64},{40,72},{48,80},{56,88},{64,... | collective-permute-start | bytes 393224 | tf_op jit(solution)/shard_map/ppermute | solution.py:67
  714.2 18.4 %collective-permute-start.5 = (bf16[512,128]{1,0:T(8,128)(2,1)S(1)}, bf16[512,128]{1,0:T(8,128)(2,1)S(1)}, u32[]{:S(2)}, u32[]{:S(2)}) collective-permute-start(bf16[512,128]{1,0:T(8,128)(2,1)S(1)} %convolution_convert_fusion.2), channel_id=1, source_target_pairs={{0,24},{8,32},{16,40},{24,48},{32,56},{40,64},{48,72},{56,80},{64,... | collective-permute-start | bytes 393224 | tf_op jit(solution)/shard_map/ppermute | solution.py:67
  717.0 17.6 %collective-permute-start.6 = (bf16[512,128]{1,0:T(8,128)(2,1)S(1)}, bf16[512,128]{1,0:T(8,128)(2,1)S(1)}, u32[]{:S(2)}, u32[]{:S(2)}) collective-permute-start(bf16[512,128]{1,0:T(8,128)(2,1)S(1)} %convolution_convert_fusion.2), channel_id=1, source_target_pairs={{0,16},{8,24},{16,32},{24,40},{32,48},{40,56},{48,64},{56,72},{64,... | collective-permute-start | bytes 393224 | tf_op jit(solution)/shard_map/ppermute | solution.py:67
  724.5 12.1 %collective-permute-start.7 = (bf16[512,128]{1,0:T(8,128)(2,1)S(1)}, bf16[512,128]{1,0:T(8,128)(2,1)S(1)}, u32[]{:S(2)}, u32[]{:S(2)}) collective-permute-start(bf16[512,128]{1,0:T(8,128)(2,1)S(1)} %convolution_convert_fusion.2), channel_id=1, source_target_pairs={{0,8},{8,16},{16,24},{24,32},{32,40},{40,48},{48,56},{56,64},{64,7... | collective-permute-start | bytes 393224 | tf_op jit(solution)/shard_map/ppermute | solution.py:67
  726.4 20.9 %collective-permute-start.8 = (bf16[512,128]{1,0:T(8,128)(2,1)S(1)}, bf16[512,128]{1,0:T(8,128)(2,1)S(1)}, u32[]{:S(2)}, u32[]{:S(2)}) collective-permute-start(bf16[512,128]{1,0:T(8,128)(2,1)S(1)} %convolution_convert_fusion.1), channel_id=1, source_target_pairs={{0,64},{8,72},{16,80},{24,88},{32,96},{40,104},{48,112},{56,120},{... | collective-permute-start | bytes 393224 | tf_op jit(solution)/shard_map/ppermute | solution.py:67
  730.7 18.6 %collective-permute-start.9 = (bf16[512,128]{1,0:T(8,128)(2,1)S(1)}, bf16[512,128]{1,0:T(8,128)(2,1)S(1)}, u32[]{:S(2)}, u32[]{:S(2)}) collective-permute-start(bf16[512,128]{1,0:T(8,128)(2,1)S(1)} %convolution_convert_fusion.1), channel_id=1, source_target_pairs={{0,56},{8,64},{16,72},{24,80},{32,88},{40,96},{48,104},{56,112},{6... | collective-permute-start | bytes 393224 | tf_op jit(solution)/shard_map/ppermute | solution.py:67
  732.7 18.6 %collective-permute-start.10 = (bf16[512,128]{1,0:T(8,128)(2,1)S(1)}, bf16[512,128]{1,0:T(8,128)(2,1)S(1)}, u32[]{:S(2)}, u32[]{:S(2)}) collective-permute-start(bf16[512,128]{1,0:T(8,128)(2,1)S(1)} %convolution_convert_fusion.1), channel_id=1, source_target_pairs={{0,48},{8,56},{16,64},{24,72},{32,80},{40,88},{48,96},{56,104},{64... | collective-permute-start | bytes 393224 | tf_op jit(solution)/shard_map/ppermute | solution.py:67
  734.6 18.8 %collective-permute-start.11 = (bf16[512,128]{1,0:T(8,128)(2,1)S(1)}, bf16[512,128]{1,0:T(8,128)(2,1)S(1)}, u32[]{:S(2)}, u32[]{:S(2)}) collective-permute-start(bf16[512,128]{1,0:T(8,128)(2,1)S(1)} %convolution_convert_fusion.1), channel_id=1, source_target_pairs={{0,40},{8,48},{16,56},{24,64},{32,72},{40,80},{48,88},{56,96},{64,... | collective-permute-start | bytes 393224 | tf_op jit(solution)/shard_map/ppermute | solution.py:67
  736.6 16.9 %collective-permute-start.12 = (bf16[512,128]{1,0:T(8,128)(2,1)S(1)}, bf16[512,128]{1,0:T(8,128)(2,1)S(1)}, u32[]{:S(2)}, u32[]{:S(2)}) collective-permute-start(bf16[512,128]{1,0:T(8,128)(2,1)S(1)} %convolution_convert_fusion.1), channel_id=1, source_target_pairs={{0,32},{8,40},{16,48},{24,56},{32,64},{40,72},{48,80},{56,88},{64,... | collective-permute-start | bytes 393224 | tf_op jit(solution)/shard_map/ppermute | solution.py:67
  747.3 10.1 %collective-permute-start.13 = (bf16[512,128]{1,0:T(8,128)(2,1)S(1)}, bf16[512,128]{1,0:T(8,128)(2,1)S(1)}, u32[]{:S(2)}, u32[]{:S(2)}) collective-permute-start(bf16[512,128]{1,0:T(8,128)(2,1)S(1)} %convolution_convert_fusion.1), channel_id=1, source_target_pairs={{0,24},{8,32},{16,40},{24,48},{32,56},{40,64},{48,72},{56,80},{64,... | collective-permute-start | bytes 393224 | tf_op jit(solution)/shard_map/ppermute | solution.py:67
  749.3 9.6 %collective-permute-start.14 = (bf16[512,128]{1,0:T(8,128)(2,1)S(1)}, bf16[512,128]{1,0:T(8,128)(2,1)S(1)}, u32[]{:S(2)}, u32[]{:S(2)}) collective-permute-start(bf16[512,128]{1,0:T(8,128)(2,1)S(1)} %convolution_convert_fusion.1), channel_id=1, source_target_pairs={{0,16},{8,24},{16,32},{24,40},{32,48},{40,56},{48,64},{56,72},{64,... | collective-permute-start | bytes 393224 | tf_op jit(solution)/shard_map/ppermute | solution.py:67
  (26 other events, 1024.0 us)
Sparse Core Ops, SparseCore 0:
  9.9 64.4 all-gather.16
  85.8 75.0 all-gather.18
  163.5 57.3 all-gather.20
  229.6 14.5 all-gather.24
  255.5 154.6 all-gather.26
  427.6 84.1 all-gather.28
  514.3 63.6 all-gather.14
  620.8 80.3 all-gather.22
where the time goes:
time: 818 us; the launch traced here: 805 us
  waiting for transfers between devices  576 us (70%)
  blocking collectives  59.4 us (7%)
  local copies, waits for them, and re-layouts  47.1 us (6%)
  matrix products  40.3 us (5%)
  starting transfers between devices  39.7 us (5%)
  other arithmetic  27 us (3%)
  between operations  15.1 us (2%)
    all_gather x3, waiting for transfers between devices, gathered_once(): both, at, found = (lax.all_gather(jnp.concatenate(lines), axis), 0, {})  234 us
    all_gather x1, waiting for transfers between devices, shards(): lax.all_gather(normalize(retrieved, norm_gain), 'head', axis=0, tiled=True)  80.5 us
    all_gather x1, waiting for transfers between devices, shards(): lax.all_gather(project(tokens, mem_key_w), 'head', axis=1, tiled=True)  64.6 us
    all_gather x1, waiting for transfers between devices, shards(): lax.all_gather(2.0 / tok_rows * (predicted - value_share), 'head', axis=0...  57.5 us
    all_gather x1, waiting for transfers between devices, shards(): lax.all_gather(project(tokens, mem_value_w), 'head', axis=1, tiled=True)  51.9 us
    all_gather x1, waiting for transfers between devices, shards(): lax.all_gather(project(tokens, mem_query_w), 'head', axis=1, tiled=True)  51.9 us
    ppermute x16, starting transfers between devices, shifted(): return lax.ppermute(value, axis, pairs)  35.4 us
    all_to_all x1, blocking collectives, sent_and_summed(): lax.all_to_all(split_up(value, dim, length), axis, 0, 0, tiled=True)  29.9 us
  transfers between devices with their start and end apart: 25, of which 14 were waited for; matrix products, arithmetic and copies ran while one was open for 6% of the time, Pallas kernels for 0%

commit v1 on v0

v1 whole, which is shorter than its diff:
```python
import jax
import jax.numpy as jnp
from jax import lax
from jax.experimental import pallas as pl
from jax.experimental.pallas import tpu as pltpu
from jax.sharding import PartitionSpec as P

MESH = pl.DeviceIdType.MESH
F32 = jnp.float32
BF16 = jnp.bfloat16
EPS = 1e-06
NS = 32
NH = 8
T = 512
W = 128
NN = (((1,), (0,)), ((), ()))
NT = (((1,), (1,)), ((), ()))


def dot(a, b, dims=NN):
    return lax.dot_general(a, b, dims, preferred_element_type=F32)


def col(b):
    return pl.ds(pl.multiple_of(b * W, W), W)


def remote(src, dst, send, recv, device):
    return pltpu.make_async_remote_copy(
        src_ref=src, dst_ref=dst, send_sem=send, recv_sem=recv, device_id=device, device_id_type=MESH
    )


class Gather:
    def __init__(self, place, buf, send, recv):
        s, y, z = place
        self.buf, self.send, self.recv = buf, send, recv
        self.up, self.down, self.far = (y + 1) % 4, (y + 3) % 4, (y + 2) % 4
        self.s, self.y, self.z = s, y, z

    def copy(self, block, sem, yy, zz):
        ref = self.buf.at[:, col(block)]
        return remote(ref, ref, self.send.at[sem], self.recv.at[sem], (self.s, yy * 2 + zz))

    def copies(self):
        s, y, z = self.s, self.y, self.z
        o = 1 - z
        return (
            self.copy(y * 2 + z, 0, y, o),
            self.copy(y * 2 + z, 1, self.up, z),
            self.copy(y * 2 + z, 2, self.down, z),
            self.copy(y * 2 + o, 3, self.up, z),
            self.copy(y * 2 + o, 4, self.down, z),
            self.copy(self.down * 2 + z, 5, self.up, z),
            self.copy(self.up * 2 + o, 6, self.down, z),
        )

    def start(self):
        self.c = self.copies()
        for k in (1, 2, 0):
            self.c[k].start()

    def relay(self):
        self.c[1].wait_recv()
        self.c[5].start()
        self.c[0].wait_recv()
        self.c[3].start()
        self.c[4].start()
        self.c[4].wait_recv()
        self.c[6].start()

    def finish(self):
        for k in (2, 3, 5, 6):
            self.c[k].wait_recv()

    def drain(self):
        for c in self.c:
            c.wait_send()


def reduce_scatter(place, part, out, land, send, recv):
    s, y, z = place
    up, down, far = (y + 1) % 4, (y + 3) % 4, (y + 2) % 4
    o = 1 - z

    def copy(k, yy, zz):
        return remote(out.at[k], land.at[k], send.at[k], recv.at[k], (s, yy * 2 + zz))

    c = (
        copy(0, up, z),
        copy(1, down, z),
        copy(2, down, z),
        copy(3, up, z),
        copy(4, up, z),
        copy(5, down, z),
        copy(6, y, o),
    )
    out[0] = part(far * 2).astype(BF16)
    c[0].start()
    out[1] = part(far * 2 + 1).astype(BF16)
    c[1].start()
    out[3] = part(up * 2 + 1).astype(BF16)
    c[3].start()
    out[2] = part(down * 2).astype(BF16)
    c[2].start()
    mine_up = part(up * 2)
    mine_down = part(down * 2 + 1)
    c[0].wait_recv()
    out[4] = (land[0].astype(F32) + mine_up).astype(BF16)
    c[4].start()
    c[1].wait_recv()
    out[5] = (land[1].astype(F32) + mine_down).astype(BF16)
    c[5].start()
    other = part(y * 2 + o)
    own = part(y * 2 + z)
    for k in (2, 3, 4, 5):
        c[k].wait_recv()
    out[6] = (other + land[2 + o].astype(F32) + land[4 + o].astype(F32)).astype(BF16)
    c[6].start()
    own = own + land[2 + z].astype(F32) + land[4 + z].astype(F32)
    c[6].wait_recv()
    own = own + land[6].astype(F32)
    return own, c


def kernel(
    tok, wq, wk, wv, m_in, m_out, fg, mo, st, plan, gain, aq, ak, av, ao, out_ref,
    kf, qf, rf, tf, cf, wo, vbuf, hid, slope, hq, mob, mot, kt,
    rs_out, rs_land, gates, gbuf, rbuf, wbuf, wland, kv, qs, nrm, m_s, l_s, acc,
    g_send, g_recv, r_send, r_recv, w_send, w_recv, gt_send, gt_recv, a_send, a_recv, b_send, b_recv, k_send, k_recv,
):
    s, h = lax.axis_index("seq"), lax.axis_index("head")
    y, z = h // 2, h % 2
    place = (s, y, z)
    par = s % 2

    barrier = pltpu.get_barrier_semaphore()

    def greet_head(d, carry):
        pl.semaphore_signal(barrier, inc=1, device_id=(s, (h + d) % NH), device_id_type=MESH)
        return carry

    def greet_seq(d, carry):
        pl.semaphore_signal(barrier, inc=1, device_id=((s + d) % NS, h), device_id_type=MESH)
        return carry

    lax.fori_loop(1, NH, greet_head, 0)
    lax.fori_loop(1, NS, greet_seq, 0)

    kf[:, col(h)] = dot(tok[...], wk[...]).astype(BF16)
    hot = lax.broadcasted_iota(jnp.int32, (16, W), 0) == plan[0]

    def row(table):
        return jnp.sum(jnp.where(hot, table[...], 0.0), axis=0, keepdims=True)

    gates[s] = jnp.concatenate([row(mo), 1.0 - row(fg), jnp.zeros((6, W), F32)], axis=0)
    rate = row(st)
    pl.semaphore_wait(barrier, NH - 1 + NS - 1)

    gk = Gather(place, kf, g_send.at[0], g_recv.at[0])
    gq = Gather(place, qf, g_send.at[1], g_recv.at[1])
    gr = Gather(place, rf, g_send.at[2], g_recv.at[2])
    gt = Gather(place, tf, g_send.at[3], g_recv.at[3])
    gc = Gather(place, cf, g_send.at[4], g_recv.at[4])
    gk.start()

    def send_gates(d, carry):
        remote(gates.at[s], gates.at[s], gt_send, gt_recv, ((s + d) % NS, h)).start()
        return carry

    lax.fori_loop(1, NS, send_gates, 0)
    qf[:, col(h)] = dot(tok[...], wq[...]).astype(BF16)
    vbuf[...] = dot(tok[...], wv[...]).astype(BF16)
    mob[...] = m_out[...].astype(BF16)
    gk.relay()
    mot[...] = m_out[...].T
    gk.finish()

    pre = dot(kf[...], m_in[...].astype(BF16))
    sig = jax.nn.sigmoid(pre)
    hid[...] = (pre * sig).astype(BF16)
    slope[...] = sig * (1.0 + pre * (1.0 - sig))

    def part_one(b):
        return dot(hid[...], mob[:, col(b)])

    predicted, sent_one = reduce_scatter(place, part_one, rs_out.at[0], rs_land.at[0], r_send.at[0], r_recv.at[0])
    rf[:, col(h)] = ((2.0 / T) * (predicted - vbuf[...].astype(F32))).astype(BF16)
    gr.start()
    kt[...] = kf[...].T
    gr.relay()
    gr.finish()

    g_out = dot(hid[...].T, rf[...])
    gbuf[:, 32:64, :] = (g_out.T * -rate).astype(BF16).reshape(NS, 32, W)
    term = (dot(rf[...], mob[...], NT) * slope[...]).astype(BF16)
    gbuf[:, 0:32, :] = (dot(kt[...], term) * -rate).astype(BF16).reshape(NS, 32, W)

    def send_grad(d, carry):
        o = (s + d) % NS
        remote(gbuf.at[o], rbuf.at[s], a_send, a_recv.at[s], (o, h)).start()
        return carry

    lax.fori_loop(1, NS, send_grad, 0)
    rbuf[s] = gbuf[s]
    gq.start()

    def wo_copy(d):
        p = (h + d) % NH
        return remote(ao.at[:, col(p)], wo.at[pl.ds(pl.multiple_of(h * W, W), W), :], w_send.at[d - 1], w_recv.at[d - 1], (s, p))

    for d in range(1, NH):
        wo_copy(d).start()
    wo[pl.ds(pl.multiple_of(h * W, W), W), :] = ao[:, col(h)]

    pltpu.make_async_copy(gates.at[pl.ds(0, NS - 1)], gates.at[pl.ds(0, NS - 1)], gt_recv).wait()

    rows = pl.ds(pl.multiple_of(s * 32, 32), 32)
    weight0 = jnp.concatenate([m_in[rows, :], mot[rows, :]], axis=0)

    def step(c, carry):
        speed, weight = carry
        wbuf[c] = weight.astype(BF16)

        @pl.when(c != s)
        def _():
            remote(wbuf.at[c], wland.at[s], b_send, b_recv, (c, h)).start()
            remote(gbuf.at[c], rbuf.at[c], a_send, a_recv.at[c], (c, h)).wait_recv()

        g = gates[c]
        speed = g[0:1] * speed + rbuf[c].astype(F32)
        weight = g[1:2] * weight + speed
        return speed, weight

    lax.fori_loop(0, NS, step, (jnp.zeros((64, W), F32), weight0))
    wland[s] = wbuf[s]
    gq.relay()
    gq.finish()
    some = pl.ds(0, NS - 1)
    pltpu.make_async_copy(wland.at[some], wland.at[some], b_recv).wait()

    act = dot(qf[...], wland[:, 0:32, :].reshape(1024, W))
    hq[...] = (act * jax.nn.sigmoid(act)).astype(BF16)

    def part_two(b):
        return dot(hq[...], wland[pl.ds(b * 4, 4), 32:64, :].reshape(W, W), NT)

    retrieved, sent_two = reduce_scatter(place, part_two, rs_out.at[1], rs_land.at[1], r_send.at[1], r_recv.at[1])
    tf[:, col(h)] = retrieved.astype(BF16)
    gt.start()
    gt.relay()
    gt.finish()
    for i in range(4):
        r = slice(i * 128, (i + 1) * 128)
        x = tf[r, :].astype(F32)
        mean = jnp.mean(x * x, axis=-1, keepdims=True)
        nrm[r, :] = (x * lax.rsqrt(mean + EPS) * gain[...]).astype(BF16)
    kv[0, :, 0:W] = dot(nrm[...], ak[...]).astype(BF16)
    kv[0, :, W : 2 * W] = dot(nrm[...], av[...]).astype(BF16)

    def own_copy(k):
        return remote(kv.at[0], kv.at[2 * k], k_send.at[k], k_recv.at[2 * k], (s + 2 * k, h))

    def side_copy():
        return remote(kv.at[0], kv.at[1], k_send.at[0], k_recv.at[1], (s + 1, h))

    def pass_copy(k):
        to = 2 * k + 1 - 2 * par
        return remote(kv.at[2 * k], kv.at[to], k_send.at[4 + k], k_recv.at[to], (s + 1 - 2 * par, h))

    def passes(k):
        return (s >= 2 * k) & ((par == 1) | (k < 4))

    for k in range(1, 5):

        @pl.when(s + 2 * k < NS)
        def _():
            own_copy(k).start()

    @pl.when(par == 0)
    def _():
        side_copy().start()

    query = dot(nrm[...], aq[...]).astype(BF16) * 0.125
    low = lax.broadcasted_iota(jnp.int32, (T, W), 1) < 64
    zero = jnp.zeros_like(query)
    qs[0] = jnp.where(low, query, zero)
    qs[1] = jnp.where(low, zero, query)
    m_s[...] = jnp.full_like(m_s, -1e30)
    l_s[...] = jnp.zeros_like(l_s)
    acc[...] = jnp.zeros_like(acc)

    def attend(slot, mode):
        for hd in range(2):
            for i in range(4):
                r = slice(i * 128, (i + 1) * 128)
                sc = dot(qs[hd, r, :], kv[slot, :, 0:W], NT)
                if mode != 1:
                    iq = lax.broadcasted_iota(jnp.int32, (128, T), 0) + i * 128
                    ik = lax.broadcasted_iota(jnp.int32, (128, T), 1)
                    sc = jnp.where(iq >= ik if mode == 0 else ik > iq, sc, -1e30)
                m_old = m_s[hd, r, :]
                m_new = jnp.maximum(m_old, jnp.max(sc, axis=-1, keepdims=True))
                p = jnp.exp(sc - m_new)
                fade = jnp.exp(m_old - m_new)
                m_s[hd, r, :] = m_new
                l_s[hd, r, :] = fade * l_s[hd, r, :] + jnp.sum(p, axis=-1, keepdims=True)
                acc[hd, r, :] = fade * acc[hd, r, :] + dot(p.astype(BF16), kv[slot, :, W : 2 * W])

    attend(0, 0)

    def arrive(slot):
        remote(kv.at[0], kv.at[slot], k_send.at[0], k_recv.at[slot], (s, h ^ 1)).wait_recv()

    def pair(k, mode):
        @pl.when(s >= 2 * k)
        def _():
            arrive(2 * k)

            @pl.when(passes(k))
            def _():
                pass_copy(k).start()

            attend(2 * k, mode)

        @pl.when(s >= 2 * k - 1)
        def _():
            arrive(2 * k - 1)
            attend(2 * k - 1, 1)

    def middle(k, carry):
        pair(k, 1)
        return carry

    lax.fori_loop(1, 4, middle, 0)
    pair(4, 2)
    cf[:, col(h)] = jnp.where(low, acc[0] / l_s[0], acc[1] / l_s[1]).astype(BF16)
    gc.start()
    gc.relay()
    for d in range(1, NH):
        wo_copy(d).wait_recv()
    gc.finish()
    out_ref[...] = dot(cf[...], wo[...]).astype(BF16)

    for g in (gk, gq, gr, gt, gc):
        g.drain()
    for c in sent_one + sent_two:
        c.wait_send()
    for d in range(1, NH):
        wo_copy(d).wait_send()
    pltpu.make_async_copy(gates.at[some], gates.at[some], gt_send).wait()
    pltpu.make_async_copy(gbuf.at[some], gbuf.at[some], a_send).wait()
    pltpu.make_async_copy(wbuf.at[some], wbuf.at[some], b_send).wait()
    for k in range(1, 5):

        @pl.when(s + 2 * k < NS)
        def _():
            own_copy(k).wait_send()

        @pl.when(passes(k))
        def _():
            pass_copy(k).wait_send()

    @pl.when(par == 0)
    def _():
        side_copy().wait_send()


def block(
    tokens, mem_query_w, mem_key_w, mem_value_w, mem_in, mem_out, forget_levels, momentum_levels, step_levels,
    plan, norm_gain, attn_query_w, attn_key_w, attn_value_w, attn_out_w,
):
    vm = pl.BlockSpec(memory_space=pltpu.VMEM)
    sm = pl.BlockSpec(memory_space=pltpu.SMEM)
    V = pltpu.VMEM
    dma = pltpu.SemaphoreType.DMA
    big = V((T, 1024), BF16)
    slab = V((NS, 64, W), BF16)
    return pl.pallas_call(
        kernel,
        name="titans",
        out_shape=jax.ShapeDtypeStruct((T, W), BF16),
        in_specs=[vm] * 9 + [sm] + [vm] * 5,
        out_specs=vm,
        scratch_shapes=[
            big, big, big, big, big,
            V((1024, W), BF16), V((T, W), BF16), V((T, W), BF16), V((T, W), F32), V((T, W), BF16),
            V((W, 1024), BF16), V((1024, W), F32), V((1024, T), BF16),
            V((2, 7, T, W), BF16), V((2, 7, T, W), BF16), V((NS, 8, W), F32),
            slab, slab, slab, slab,
            V((9, T, 2 * W), BF16), V((2, T, W), BF16), big, V((2, T, 1), F32), V((2, T, 1), F32), V((2, T, W), F32),
            dma((5, 7)), dma((5, 7)), dma((2, 7)), dma((2, 7)), dma((7,)), dma((7,)), dma, dma,
            dma, dma((NS,)), dma, dma, dma((9,)), dma((9,)),
        ],
        compiler_params=pltpu.CompilerParams(collective_id=0, has_side_effects=True, vmem_limit_bytes=60 * 1024 * 1024),
    )(
        tokens, mem_query_w, mem_key_w, mem_value_w, mem_in, mem_out, forget_levels, momentum_levels, step_levels,
        plan, norm_gain.reshape(1, -1), attn_query_w, attn_key_w, attn_value_w, attn_out_w,
    )


def solution(mesh):
    seq, head = P("seq", None), P(None, "head")
    in_specs = (
        seq, head, head, head, head, P("head", None), head, head, head, P("seq"), P(), head, head, head, P("head", None),
    )
    return jax.shard_map(block, mesh=mesh, in_specs=in_specs, out_specs=P("seq", "head"), check_vma=False)
```

time: 818 us -> 198 us (0.24)
  the two profiles are of different devices: /device:TPU:6 before, /device:TPU:76 now
where the time goes in v1:
time: 198 us
  Pallas kernels  196 us (99%)
    pallas_call x1, Pallas kernels, block(): pl.pallas_call(kernel, name='titans', out_shape=jax.ShapeDtypeStruct((T,...  196 us

profile of v1, /device:TPU:76, one launch (start us, length us, event | category | flops | bytes accessed | tf_op | source)
XLA Modules:
  0.0 197.9 jit_solution(16688886367189261362)
XLA Ops:
  0.7 195.6 %titans.1 = bf16[512,128]{1,0:T(8,128)(2,1)} custom-call(bf16[512,1024]{1,0:T(8,128)(2,1)} %tok.1, bf16[1024,128]{1,0:T(8,128)(2,1)} %wq.1, bf16[1024,128]{1,0:T(8,128)(2,1)} %wk.1, bf16[1024,128]{1,0:T(8,128)(2,1)} %wv.1, f32[1024,128]{1,0:T(8,128)} %m_in.1, f32[128,1024]{1,0:T(8,128)} %m_out.1, f32[16,128]{1,0:T(8,128)} %fg.1, f32[16,128]{1,0:T(8,128)} %mo.1, ...), custom_call_target="tpu_custom_call" | custom-call | tf_op jit(solution)/shard_map/titans/pallas_call | solution.py:379
  196.3 1.6 copy.18

commit v2 on v1

--- a/solution.py
+++ b/solution.py
@@ -60,14 +60,20 @@
         for k in (1, 2, 0):
             self.c[k].start()
 
-    def relay(self):
+    def relay_near(self):
         self.c[1].wait_recv()
         self.c[5].start()
         self.c[0].wait_recv()
         self.c[3].start()
         self.c[4].start()
+
+    def relay_far(self):
         self.c[4].wait_recv()
         self.c[6].start()
+
+    def relay(self):
+        self.relay_near()
+        self.relay_far()
 
     def finish(self):
         for k in (2, 3, 5, 6):
@@ -126,7 +132,7 @@
 def kernel(
     tok, wq, wk, wv, m_in, m_out, fg, mo, st, plan, gain, aq, ak, av, ao, out_ref,
     kf, qf, rf, tf, cf, wo, vbuf, hid, slope, hq, mob, mot, kt,
-    rs_out, rs_land, gates, gbuf, rbuf, wbuf, wland, kv, qs, nrm, m_s, l_s, acc,
+    rs_out, rs_land, gates, gbuf, rbuf, wbuf, wland, kv, qs, nrm, m_s, acc,
     g_send, g_recv, r_send, r_recv, w_send, w_recv, gt_send, gt_recv, a_send, a_recv, b_send, b_recv, k_send, k_recv,
 ):
     s, h = lax.axis_index("seq"), lax.axis_index("head")
@@ -189,6 +195,7 @@
     gr.start()
     kt[...] = kf[...].T
     gr.relay()
+    gq.start()
     gr.finish()
 
     g_out = dot(hid[...].T, rf[...])
@@ -203,7 +210,6 @@
 
     lax.fori_loop(1, NS, send_grad, 0)
     rbuf[s] = gbuf[s]
-    gq.start()
 
     def wo_copy(d):
         p = (h + d) % NH
@@ -232,9 +238,12 @@
         weight = g[1:2] * weight + speed
         return speed, weight
 
-    lax.fori_loop(0, NS, step, (jnp.zeros((64, W), F32), weight0))
+    state = lax.fori_loop(0, 4, step, (jnp.zeros((64, W), F32), weight0))
+    gq.relay_near()
+    state = lax.fori_loop(4, 20, step, state)
+    gq.relay_far()
+    lax.fori_loop(20, NS, step, state)
     wland[s] = wbuf[s]
-    gq.relay()
     gq.finish()
     some = pl.ds(0, NS - 1)
     pltpu.make_async_copy(wland.at[some], wland.at[some], b_recv).wait()
@@ -258,6 +267,8 @@
     kv[0, :, 0:W] = dot(nrm[...], ak[...]).astype(BF16)
     kv[0, :, W : 2 * W] = dot(nrm[...], av[...]).astype(BF16)
 
+    zl = (s // 2) % 4
+
     def own_copy(k):
         return remote(kv.at[0], kv.at[2 * k], k_send.at[k], k_recv.at[2 * k], (s + 2 * k, h))
 
@@ -268,12 +279,24 @@
         to = 2 * k + 1 - 2 * par
         return remote(kv.at[2 * k], kv.at[to], k_send.at[4 + k], k_recv.at[to], (s + 1 - 2 * par, h))
 
+    def relay_copy(up):
+        to = 6 if up else 2
+        return remote(kv.at[4], kv.at[to], k_send.at[9], k_recv.at[to], (s + 2 if up else s - 2, h))
+
+    def sends(k):
+        ok = s + 2 * k < NS
+        if k == 3:
+            ok = ok & (zl != 0)
+        if k == 1:
+            ok = ok & (zl != 3)
+        return ok
+
     def passes(k):
         return (s >= 2 * k) & ((par == 1) | (k < 4))
 
-    for k in range(1, 5):
-
-        @pl.when(s + 2 * k < NS)
+    for k in (2, 1, 3, 4):
+
+        @pl.when(sends(k))
         def _():
             own_copy(k).start()
 
@@ -282,59 +305,71 @@
         side_copy().start()
 
     query = dot(nrm[...], aq[...]).astype(BF16) * 0.125
-    low = lax.broadcasted_iota(jnp.int32, (T, W), 1) < 64
-    zero = jnp.zeros_like(query)
-    qs[0] = jnp.where(low, query, zero)
-    qs[1] = jnp.where(low, zero, query)
+    low = lax.broadcasted_iota(jnp.int32, (128, W), 1) < 64
+    for i in range(4):
+        part = query[i * 128 : (i + 1) * 128, :]
+        qs[i, 0:128, :] = jnp.where(low, part, jnp.zeros_like(part))
+        qs[i, 128:256, :] = jnp.where(low, jnp.zeros_like(part), part)
     m_s[...] = jnp.full_like(m_s, -1e30)
-    l_s[...] = jnp.zeros_like(l_s)
     acc[...] = jnp.zeros_like(acc)
-
-    def attend(slot, mode):
-        for hd in range(2):
-            for i in range(4):
-                r = slice(i * 128, (i + 1) * 128)
-                sc = dot(qs[hd, r, :], kv[slot, :, 0:W], NT)
-                if mode != 1:
-                    iq = lax.broadcasted_iota(jnp.int32, (128, T), 0) + i * 128
-                    ik = lax.broadcasted_iota(jnp.int32, (128, T), 1)
-                    sc = jnp.where(iq >= ik if mode == 0 else ik > iq, sc, -1e30)
-                m_old = m_s[hd, r, :]
-                m_new = jnp.maximum(m_old, jnp.max(sc, axis=-1, keepdims=True))
-                p = jnp.exp(sc - m_new)
-                fade = jnp.exp(m_old - m_new)
-                m_s[hd, r, :] = m_new
-                l_s[hd, r, :] = fade * l_s[hd, r, :] + jnp.sum(p, axis=-1, keepdims=True)
-                acc[hd, r, :] = fade * acc[hd, r, :] + dot(p.astype(BF16), kv[slot, :, W : 2 * W])
+    ones = jnp.ones((T, W), BF16)
+
+    def attend(slot, mode, edge=None):
+        values = jnp.concatenate([kv[slot, :, W : 2 * W], ones], axis=1)
+        for i in range(4):
+            sc = dot(qs[i], kv[slot, :, 0:W], NT)
+            if mode != 1:
+                iq = lax.broadcasted_iota(jnp.int32, (256, T), 0) % 128 + i * 128
+                ik = lax.broadcasted_iota(jnp.int32, (256, T), 1)
+                sc = jnp.where(iq >= ik if mode == 0 else ik - iq > edge, sc, -1e30)
+            m_old = m_s[i]
+            m_new = jnp.maximum(m_old, jnp.max(sc, axis=-1, keepdims=True))
+            p = jnp.exp(sc - m_new)
+            m_s[i] = m_new
+            acc[i] = jnp.exp(m_old - m_new) * acc[i] + dot(p.astype(BF16), values)
 
     attend(0, 0)
-
     def arrive(slot):
         remote(kv.at[0], kv.at[slot], k_send.at[0], k_recv.at[slot], (s, h ^ 1)).wait_recv()
 
-    def pair(k, mode):
-        @pl.when(s >= 2 * k)
+    last = jnp.where(zl == 0, 1, 3)
+
+    def chip(j):
+        return jnp.where(j == 0, 2, jnp.where(j == 1, 4, jnp.where(j == 2, 4 - last, last)))
+
+    def turn(j, carry):
+        k = chip(j)
+        odd = jnp.where(j == 0, par, 2 * chip(j - 1) - 1 + 2 * par)
+
+        @pl.when((j < 4) & (s >= 2 * k))
         def _():
             arrive(2 * k)
+
+            @pl.when((k == 2) & (zl == 2))
+            def _():
+                relay_copy(True).start()
+
+            @pl.when((k == 2) & (zl == 1))
+            def _():
+                relay_copy(False).start()
 
             @pl.when(passes(k))
             def _():
                 pass_copy(k).start()
 
-            attend(2 * k, mode)
-
-        @pl.when(s >= 2 * k - 1)
-        def _():
-            arrive(2 * k - 1)
-            attend(2 * k - 1, 1)
-
-    def middle(k, carry):
-        pair(k, 1)
+            attend(2 * k, 2, jnp.where(k == 4, 0, -2 * T))
+
+        @pl.when((odd > 0) & (odd < 9) & (s >= odd))
+        def _():
+            arrive(odd)
+            attend(odd, 1)
+
         return carry
 
-    lax.fori_loop(1, 4, middle, 0)
-    pair(4, 2)
-    cf[:, col(h)] = jnp.where(low, acc[0] / l_s[0], acc[1] / l_s[1]).astype(BF16)
+    lax.fori_loop(0, 5, turn, 0)
+    for i in range(4):
+        both = acc[i, :, 0:W] / acc[i, :, W : 2 * W]
+        cf[i * 128 : (i + 1) * 128, col(h)] = jnp.where(low, both[0:128], both[128:256]).astype(BF16)
     gc.start()
     gc.relay()
     for d in range(1, NH):
@@ -353,7 +388,7 @@
     pltpu.make_async_copy(wbuf.at[some], wbuf.at[some], b_send).wait()
     for k in range(1, 5):
 
-        @pl.when(s + 2 * k < NS)
+        @pl.when(sends(k))
         def _():
             own_copy(k).wait_send()
 
@@ -364,6 +399,14 @@
     @pl.when(par == 0)
     def _():
         side_copy().wait_send()
+
+    @pl.when((s >= 4) & (zl == 2))
+    def _():
+        relay_copy(True).wait_send()
+
+    @pl.when((s >= 4) & (zl == 1))
+    def _():
+        relay_copy(False).wait_send()
 
 
 def block(
@@ -388,9 +431,9 @@
             V((W, 1024), BF16), V((1024, W), F32), V((1024, T), BF16),
             V((2, 7, T, W), BF16), V((2, 7, T, W), BF16), V((NS, 8, W), F32),
             slab, slab, slab, slab,
-            V((9, T, 2 * W), BF16), V((2, T, W), BF16), big, V((2, T, 1), F32), V((2, T, 1), F32), V((2, T, W), F32),
+            V((9, T, 2 * W), BF16), V((4, 256, W), BF16), big, V((4, 256, 1), F32), V((4, 256, 2 * W), F32),
             dma((5, 7)), dma((5, 7)), dma((2, 7)), dma((2, 7)), dma((7,)), dma((7,)), dma, dma,
-            dma, dma((NS,)), dma, dma, dma((9,)), dma((9,)),
+            dma, dma((NS,)), dma, dma, dma((10,)), dma((9,)),
         ],
         compiler_params=pltpu.CompilerParams(collective_id=0, has_side_effects=True, vmem_limit_bytes=60 * 1024 * 1024),
     )(

time: 198 us -> 177 us (0.89)
  the two profiles are of different devices: /device:TPU:76 before, /device:TPU:6 now
where the time goes in v2:
time: 177 us; the launch traced here: 176 us
  Pallas kernels  174 us (98%)
    pallas_call x1, Pallas kernels, block(): pl.pallas_call(kernel, name='titans', out_shape=jax.ShapeDtypeStruct((T,...  174 us

profile of v2, /device:TPU:6, one launch (start us, length us, event | category | flops | bytes accessed | tf_op | source)
XLA Modules:
  0.0 176.3 jit_solution(3592528922180847443)
XLA Ops:
  0.7 174.1 %titans.1 = bf16[512,128]{1,0:T(8,128)(2,1)} custom-call(bf16[512,1024]{1,0:T(8,128)(2,1)} %tok.1, bf16[1024,128]{1,0:T(8,128)(2,1)} %wq.1, bf16[1024,128]{1,0:T(8,128)(2,1)} %wk.1, bf16[1024,128]{1,0:T(8,128)(2,1)} %wv.1, f32[1024,128]{1,0:T(8,128)} %m_in.1, f32[128,1024]{1,0:T(8,128)} %m_out.1, f32[16,128]{1,0:T(8,128)} %fg.1, f32[16,128]{1,0:T(8,128)} %mo.1, ...), custom_call_target="tpu_custom_call" | custom-call | tf_op jit(solution)/shard_map/titans/pallas_call | solution.py:422
  174.7 1.6 copy.18

commit v3 on v2

v3 whole, which is shorter than its diff:
```python
import jax
import jax.numpy as jnp
from jax import lax
from jax.experimental import pallas as pl
from jax.experimental.pallas import tpu as pltpu
from jax.sharding import PartitionSpec as P

MESH = pl.DeviceIdType.MESH
F32 = jnp.float32
BF16 = jnp.bfloat16
EPS = 1e-06
NS = 32
NH = 8
T = 512
W = 128
NN = (((1,), (0,)), ((), ()))
NT = (((1,), (1,)), ((), ()))


def dot(a, b, dims=NN):
    return lax.dot_general(a, b, dims, preferred_element_type=F32)


def col(b):
    return pl.ds(pl.multiple_of(b * W, W), W)


def remote(src, dst, send, recv, device):
    return pltpu.make_async_remote_copy(
        src_ref=src, dst_ref=dst, send_sem=send, recv_sem=recv, device_id=device, device_id_type=MESH
    )


HALF = T // 2
PARTS = 2


def half(c):
    return pl.ds(c * HALF, HALF)


class Ring:
    def __init__(self, place, bit, buf, send, recv):
        self.s, self.y, self.z = place
        self.a, self.b = bit, 1 - bit
        self.buf, self.send, self.recv = buf, send, recv

    def copy(self, c, k):
        y, a, b = self.y, self.a, self.b
        up, down = (y + 1) % 4, (y + 3) % 4
        block, to = ((y * 2 + a, up), (y * 2 + a, down), (y * 2 + b, up), (y * 2 + b, down), (down * 2 + a, up), (up * 2 + b, down))[k]
        ref = self.buf.at[half(c), col(block)]
        return remote(ref, ref, self.send.at[c, k], self.recv.at[c, k], (self.s, to * 2 + self.z))

    def give_a(self, c):
        self.copy(c, 0).start()
        self.copy(c, 1).start()

    def give_b(self, c):
        self.copy(c, 2).start()
        self.copy(c, 3).start()

    def relay(self, c):
        self.copy(c, 0).wait_recv()
        self.copy(c, 4).start()
        self.copy(c, 3).wait_recv()
        self.copy(c, 5).start()

    def finish(self, c):
        for k in (1, 2, 4, 5):
            self.copy(c, k).wait_recv()

    def drain(self):
        for c in range(PARTS):
            for k in range(6):
                self.copy(c, k).wait_send()


class Core:
    def __init__(self, place):
        self.s, self.y, self.z = place
        self.k = self.s % 2
        up, down = (self.y + 1) % 4, (self.y + 3) % 4
        self.far = (self.y + 2) % 4
        self.next = jnp.where(self.k == 0, up, down)
        self.prev = jnp.where(self.k == 0, down, up)

    def at(self, y):
        return (self.s, y * 2 + self.z)

    def other(self):
        return (self.s + 1 - 2 * self.k, self.y * 2 + self.z)


def gather(core, buf, send, recv):
    me, k = core, core.k

    def copy(n, y, to):
        ref = buf.at[:, col(y * 2 + k)]
        return remote(ref, ref, send.at[n], recv.at[n], to)

    c = (
        copy(0, me.y, me.at(me.next)),
        copy(1, me.y, me.at(me.prev)),
        copy(2, me.prev, me.at(me.next)),
        copy(3, me.y, me.other()),
        copy(4, me.prev, me.other()),
        copy(5, me.next, me.other()),
        copy(6, me.far, me.other()),
    )

    def start():
        for n in (0, 1, 3):
            c[n].start()

    def finish():
        c[0].wait_recv()
        c[2].start()
        c[4].start()
        c[1].wait_recv()
        c[5].start()
        c[2].wait_recv()
        c[6].start()
        for n in (3, 4, 5, 6):
            c[n].wait_recv()

    return start, finish, c


def reduce_scatter(core, part, out, land, send, recv):
    me, k = core, core.k

    def copy(n, to):
        return remote(out.at[n], land.at[n], send.at[n], recv.at[n], to)

    order = (me.far, me.next, me.prev, me.y)
    c = tuple(copy(n, me.other()) for n in range(4)) + (copy(4, me.at(me.next)), copy(5, me.at(me.next)), copy(6, me.at(me.prev)))
    slot = (0, 2, 1, 3)
    for n, y in enumerate(order):
        out[n] = part(y * 2 + 1 - k).astype(BF16)
        c[n].start()

    def chip(n):
        mine = part(order[n] * 2 + k)
        c[slot[n]].wait_recv()
        return mine + land[slot[n]].astype(F32)

    out[4] = chip(0).astype(BF16)
    c[4].start()
    out[6] = chip(2).astype(BF16)
    c[6].start()
    onward = chip(1)
    own = chip(3)
    c[4].wait_recv()
    out[5] = (land[4].astype(F32) + onward).astype(BF16)
    c[5].start()
    c[6].wait_recv()
    own = own + land[6].astype(F32)
    c[5].wait_recv()
    return own + land[5].astype(F32), c


def kernel(
    tok, wq, wk, wv, m_in, m_out, fg, mo, st, plan, gain, aq, ak, av, ao, out_ref,
    kf, qf, rf, tf, cf, wo, kb, qb, vb, tb, vbuf, hid, slope, hq, mi, mob, mot, w0, w0s, kt,
    rs_out, rs_land, gates, gown, gbuf, rbuf, wbuf, wland, kv, qs, nrm, m_s, acc,
    g_send, g_recv, h_send, h_recv, r_send, r_recv, p_send, p_recv, w_send, w_recv, gt_send, gt_recv,
    a_send, a_recv, b_send, b_recv, k_send, k_recv,
):
    s, h = lax.axis_index("seq"), lax.axis_index("head")
    y, z = h // 2, h % 2
    place = (s, y, z)
    par = s % 2
    home = par == z
    away = par != z
    g = s - par + z
    core = Core(place)
    across = (s, y * 2 + 1 - z)
    aside = core.other()
    pair = (s + 1 - 2 * par, y * 2 + 1 - z)

    def group(c):
        return (c // 2 * 2 + par, y * 2 + c % 2)

    def send(n, src, dst, to):
        return remote(src, dst, p_send.at[n], p_recv.at[n], to)

    barrier = pltpu.get_barrier_semaphore()

    def greet_head(d, carry):
        pl.semaphore_signal(barrier, inc=1, device_id=(s, (h + d) % NH), device_id_type=MESH)
        return carry

    def greet_seq(d, carry):
        pl.semaphore_signal(barrier, inc=1, device_id=group((g + d) % NS), device_id_type=MESH)
        return carry

    lax.fori_loop(1, NH, greet_head, 0)
    lax.fori_loop(1, NS, greet_seq, 0)
    for to in (aside, pair):
        pl.semaphore_signal(barrier, inc=1, device_id=to, device_id_type=MESH)

    key = dot(tok[...], wk[...]).astype(BF16)
    kb[...] = key

    @pl.when(home)
    def _():
        kf[:, col(h)] = key

    hot = lax.broadcasted_iota(jnp.int32, (16, W), 0) == plan[0]

    def row(table):
        return jnp.sum(jnp.where(hot, table[...], 0.0), axis=0, keepdims=True)

    gown[...] = jnp.concatenate([row(mo), 1.0 - row(fg), row(st), jnp.zeros((5, W), F32)], axis=0)
    pl.semaphore_wait(barrier, NH - 1 + NS - 1 + 2)

    ring_k = Ring(place, z, kf, g_send.at[0], g_recv.at[0])
    ring_q = Ring(place, z, qf, g_send.at[1], g_recv.at[1])
    ring_t = Ring(place, par, tf, g_send.at[2], g_recv.at[2])
    ring_c = Ring(place, z, cf, g_send.at[3], g_recv.at[3])

    def z_copy(n, c, src, dst):
        return send(n + c, src.at[half(c)], dst.at[half(c), col(h)], across)

    def side_rows(n, c, buf):
        return send(n + c, buf.at[half(c)], buf.at[half(c)], aside)

    def v_copy():
        return send(4, vb, vbuf, pair)

    def gate_copy():
        return send(5, gown, gates.at[s], pair)

    def mi_copy():
        return send(6, mi, mi, across)

    def mo_copy():
        return send(7, mob, mob, across)

    def w0_copy():
        return send(8, w0s, w0, across)

    @pl.when(home)
    def _():
        for c in range(PARTS):
            ring_k.give_a(c)
        mi[...] = m_in[...].astype(BF16)
        mob[...] = m_out[...].astype(BF16)

    @pl.when(away)
    def _():
        for c in range(PARTS):
            z_copy(0, c, kb, kf).start()

    query = dot(tok[...], wq[...]).astype(BF16)
    qb[...] = query
    value = dot(tok[...], wv[...]).astype(BF16)

    @pl.when(home)
    def _():
        mi_copy().start()
        mo_copy().start()
        mot[...] = m_out[...].T
        qf[:, col(h)] = query
        vbuf[...] = value
        gates[g] = gown[...]

        def rows(c):
            r = pl.ds(pl.multiple_of(c * 32, 32), 32)
            return jnp.concatenate([m_in[r, :], mot[r, :]], axis=0)

        w0[...] = rows(g)
        w0s[...] = rows(g + 1 - 2 * z)
        w0_copy().start()

    @pl.when(away)
    def _():
        vb[...] = value
        v_copy().start()
        gate_copy().start()

    @pl.when(home)
    def _():
        for c in range(PARTS):
            z_copy(0, c, kb, kf).wait_recv()
            ring_k.give_b(c)
        for c in range(PARTS):
            ring_k.relay(c)
        for c in range(PARTS):
            ring_k.finish(c)
            side_rows(9, c, kf).start()

    @pl.when(away)
    def _():
        mi_copy().wait_recv()
        mo_copy().wait_recv()
        for c in range(PARTS):
            side_rows(9, c, kf).wait_recv()
        for c in range(PARTS):
            z_copy(2, c, qb, qf).start()

    pre = dot(kf[...], mi[...])
    sig = jax.nn.sigmoid(pre)
    hid[...] = (pre * sig).astype(BF16)
    slope[...] = sig * (1.0 + pre * (1.0 - sig))

    def part_one(b):
        return dot(hid[...], mob[:, col(b)])

    predicted, sent_one = reduce_scatter(core, part_one, rs_out.at[0], rs_land.at[0], r_send.at[0], r_recv.at[0])

    @pl.when(away)
    def _():
        v_copy().wait_recv()
        gate_copy().wait_recv()
        w0_copy().wait_recv()

    own = core.y * 2 + par
    rf[:, col(own)] = ((2.0 / T) * (predicted - vbuf[...].astype(F32))).astype(BF16)
    r_start, r_finish, sent_r = gather(core, rf, h_send, h_recv)
    r_start()

    def send_gates(d, carry):
        remote(gates.at[g], gates.at[g], gt_send, gt_recv, group((g + d) % NS)).start()
        return carry

    lax.fori_loop(1, NS, send_gates, 0)
    kt[...] = kf[...].T
    r_finish()

    @pl.when(home)
    def _():
        for c in range(PARTS):
            ring_q.give_a(c)

    rate = gates[g][2:3]
    g_out = dot(hid[...].T, rf[...])
    gbuf[:, 32:64, :] = (g_out.T * -rate).astype(BF16).reshape(NS, 32, W)
    term = (dot(rf[...], mob[...], NT) * slope[...]).astype(BF16)
    gbuf[:, 0:32, :] = (dot(kt[...], term) * -rate).astype(BF16).reshape(NS, 32, W)

    def send_grad(d, carry):
        o = (g + d) % NS
        remote(gbuf.at[o], rbuf.at[g], a_send, a_recv.at[g], group(o)).start()
        return carry

    lax.fori_loop(1, NS, send_grad, 0)
    rbuf[g] = gbuf[g]

    def wo_copy(d):
        p = (h + d) % NH
        return remote(ao.at[:, col(p)], wo.at[pl.ds(pl.multiple_of(h * W, W), W), :], w_send.at[d - 1], w_recv.at[d - 1], (s, p))

    for d in range(1, NH):
        wo_copy(d).start()
    wo[pl.ds(pl.multiple_of(h * W, W), W), :] = ao[:, col(h)]

    pltpu.make_async_copy(gates.at[pl.ds(0, NS - 1)], gates.at[pl.ds(0, NS - 1)], gt_recv).wait()

    def step(c, carry):
        speed, weight = carry
        wbuf[c] = weight.astype(BF16)

        @pl.when(c != g)
        def _():
            remote(wbuf.at[c], wland.at[g], b_send, b_recv, group(c)).start()
            remote(gbuf.at[c], rbuf.at[c], a_send, a_recv.at[c], group(c)).wait_recv()

        gate = gates[c]
        speed = gate[0:1] * speed + rbuf[c].astype(F32)
        weight = gate[1:2] * weight + speed
        return speed, weight

    state = lax.fori_loop(0, 4, step, (jnp.zeros((64, W), F32), w0[...]))

    @pl.when(home)
    def _():
        for c in range(PARTS):
            z_copy(2, c, qb, qf).wait_recv()
            ring_q.give_b(c)

    state = lax.fori_loop(4, 20, step, state)

    @pl.when(home)
    def _():
        for c in range(PARTS):
            ring_q.relay(c)

    lax.fori_loop(20, NS, step, state)
    wland[g] = wbuf[g]
    @pl.when(home)
    def _():
        for c in range(PARTS):
            ring_q.finish(c)
            side_rows(11, c, qf).start()

    @pl.when(away)
    def _():
        for c in range(PARTS):
            side_rows(11, c, qf).wait_recv()

    some = pl.ds(0, NS - 1)
    pltpu.make_async_copy(wland.at[some], wland.at[some], b_recv).wait()

    act = dot(qf[...], wland[:, 0:32, :].reshape(1024, W))
    hq[...] = (act * jax.nn.sigmoid(act)).astype(BF16)

    def part_two(b):
        return dot(hq[...], wland[pl.ds(b * 4, 4), 32:64, :].reshape(W, W), NT)

    retrieved, sent_two = reduce_scatter(core, part_two, rs_out.at[1], rs_land.at[1], r_send.at[1], r_recv.at[1])

    tb[...] = retrieved.astype(BF16)

    def t_copy(n, c, to):
        return send(n + c, tb.at[half(c)], tf.at[half(c), col(own)], to)

    @pl.when(home)
    def _():
        for c in range(PARTS):
            t_copy(13, c, across).start()
        tf[:, col(own)] = tb[...]
        for c in range(PARTS):
            ring_t.give_a(c)
        for c in range(PARTS):
            t_copy(17, c, aside).wait_recv()
            ring_t.give_b(c)

    @pl.when(away)
    def _():
        for c in range(PARTS):
            t_copy(17, c, aside).start()
            t_copy(15, c, pair).start()
        for c in range(PARTS):
            t_copy(13, c, across).wait_recv()
            ring_t.give_a(c)
            t_copy(15, c, pair).wait_recv()
            ring_t.give_b(c)

    for c in range(PARTS):
        ring_t.relay(c)
    for c in range(PARTS):
        ring_t.finish(c)
    for i in range(4):
        r = slice(i * 128, (i + 1) * 128)
        x = tf[r, :].astype(F32)
        mean = jnp.mean(x * x, axis=-1, keepdims=True)
        nrm[r, :] = (x * lax.rsqrt(mean + EPS) * gain[...]).astype(BF16)
    kv[0, :, 0:W] = dot(nrm[...], ak[...]).astype(BF16)
    kv[0, :, W : 2 * W] = dot(nrm[...], av[...]).astype(BF16)

    zl = (s // 2) % 4

    def own_copy(k):
        return remote(kv.at[0], kv.at[2 * k], k_send.at[k], k_recv.at[2 * k], (s + 2 * k, h))

    def side_copy():
        return remote(kv.at[0], kv.at[1], k_send.at[0], k_recv.at[1], (s + 1, h))

    def pass_copy(k):
        to = 2 * k + 1 - 2 * par
        return remote(kv.at[2 * k], kv.at[to], k_send.at[4 + k], k_recv.at[to], (s + 1 - 2 * par, h))

    def relay_copy(up):
        to = 6 if up else 2
        return remote(kv.at[4], kv.at[to], k_send.at[9], k_recv.at[to], (s + 2 if up else s - 2, h))

    def sends(k):
        ok = s + 2 * k < NS
        if k == 3:
            ok = ok & (zl != 0)
        if k == 1:
            ok = ok & (zl != 3)
        return ok

    def passes(k):
        return (s >= 2 * k) & ((par == 1) | (k < 4))

    for k in (2, 1, 3, 4):

        @pl.when(sends(k))
        def _():
            own_copy(k).start()

    @pl.when(par == 0)
    def _():
        side_copy().start()

    query = dot(nrm[...], aq[...]).astype(BF16) * 0.125
    low = lax.broadcasted_iota(jnp.int32, (128, W), 1) < 64
    for i in range(4):
        part = query[i * 128 : (i + 1) * 128, :]
        qs[i, 0:128, :] = jnp.where(low, part, jnp.zeros_like(part))
        qs[i, 128:256, :] = jnp.where(low, jnp.zeros_like(part), part)
    m_s[...] = jnp.full_like(m_s, -1e30)
    acc[...] = jnp.zeros_like(acc)
    ones = jnp.ones((T, W), BF16)

    def attend(slot, mode, edge=None):
        values = jnp.concatenate([kv[slot, :, W : 2 * W], ones], axis=1)
        for i in range(4):
            sc = dot(qs[i], kv[slot, :, 0:W], NT)
            if mode != 1:
                iq = lax.broadcasted_iota(jnp.int32, (256, T), 0) % 128 + i * 128
                ik = lax.broadcasted_iota(jnp.int32, (256, T), 1)
                sc = jnp.where(iq >= ik if mode == 0 else ik - iq > edge, sc, -1e30)
            m_old = m_s[i]
            m_new = jnp.maximum(m_old, jnp.max(sc, axis=-1, keepdims=True))
            p = jnp.exp(sc - m_new)
            m_s[i] = m_new
            acc[i] = jnp.exp(m_old - m_new) * acc[i] + dot(p.astype(BF16), values)

    attend(0, 0)
    def arrive(slot):
        remote(kv.at[0], kv.at[slot], k_send.at[0], k_recv.at[slot], (s, h ^ 1)).wait_recv()

    last = jnp.where(zl == 0, 1, 3)

    def chip(j):
        return jnp.where(j == 0, 2, jnp.where(j == 1, 4, jnp.where(j == 2, 4 - last, last)))

    def turn(j, carry):
        k = chip(j)
        odd = jnp.where(j == 0, par, 2 * chip(j - 1) - 1 + 2 * par)

        @pl.when((j < 4) & (s >= 2 * k))
        def _():
            arrive(2 * k)

            @pl.when((k == 2) & (zl == 2))
            def _():
                relay_copy(True).start()

            @pl.when((k == 2) & (zl == 1))
            def _():
                relay_copy(False).start()

            @pl.when(passes(k))
            def _():
                pass_copy(k).start()

            attend(2 * k, 2, jnp.where(k == 4, 0, -2 * T))

        @pl.when((odd > 0) & (odd < 9) & (s >= odd))
        def _():
            arrive(odd)
            attend(odd, 1)

        return carry

    lax.fori_loop(0, 5, turn, 0)
    for i in range(4):
        both = acc[i, :, 0:W] / acc[i, :, W : 2 * W]
        cf[i * 128 : (i + 1) * 128, col(h)] = jnp.where(low, both[0:128], both[128:256]).astype(BF16)

    def c_copy(c):
        ref = cf.at[half(c), col(h)]
        return send(19 + c, ref, ref, across)

    for c in range(PARTS):
        c_copy(c).start()
        ring_c.give_a(c)
    for c in range(PARTS):
        c_copy(c).wait_recv()
        ring_c.give_b(c)
    for d in range(1, NH):
        wo_copy(d).wait_recv()
    for c in range(PARTS):
        ring_c.relay(c)
    for c in range(PARTS):
        ring_c.finish(c)
        out_ref[half(c), :] = dot(cf[half(c), :], wo[...]).astype(BF16)

    @pl.when(home)
    def _():
        ring_k.drain()
        ring_q.drain()
        for c in range(PARTS):
            side_rows(9, c, kf).wait_send()
            side_rows(11, c, qf).wait_send()
            t_copy(13, c, across).wait_send()
        mi_copy().wait_send()
        mo_copy().wait_send()
        w0_copy().wait_send()

    @pl.when(away)
    def _():
        for c in range(PARTS):
            z_copy(0, c, kb, kf).wait_send()
            z_copy(2, c, qb, qf).wait_send()
            t_copy(17, c, aside).wait_send()
            t_copy(15, c, pair).wait_send()
        v_copy().wait_send()
        gate_copy().wait_send()

    ring_t.drain()
    ring_c.drain()
    for c in range(PARTS):
        c_copy(c).wait_send()
    for c in sent_one + sent_two + sent_r:
        c.wait_send()
    for d in range(1, NH):
        wo_copy(d).wait_send()
    pltpu.make_async_copy(gates.at[some], gates.at[some], gt_send).wait()
    pltpu.make_async_copy(gbuf.at[some], gbuf.at[some], a_send).wait()
    pltpu.make_async_copy(wbuf.at[some], wbuf.at[some], b_send).wait()
    for k in range(1, 5):

        @pl.when(sends(k))
        def _():
            own_copy(k).wait_send()

        @pl.when(passes(k))
        def _():
            pass_copy(k).wait_send()

    @pl.when(par == 0)
    def _():
        side_copy().wait_send()

    @pl.when((s >= 4) & (zl == 2))
    def _():
        relay_copy(True).wait_send()

    @pl.when((s >= 4) & (zl == 1))
    def _():
        relay_copy(False).wait_send()


def block(
    tokens, mem_query_w, mem_key_w, mem_value_w, mem_in, mem_out, forget_levels, momentum_levels, step_levels,
    plan, norm_gain, attn_query_w, attn_key_w, attn_value_w, attn_out_w,
):
    vm = pl.BlockSpec(memory_space=pltpu.VMEM)
    sm = pl.BlockSpec(memory_space=pltpu.SMEM)
    V = pltpu.VMEM
    dma = pltpu.SemaphoreType.DMA
    big = V((T, 1024), BF16)
    slab = V((NS, 64, W), BF16)
    return pl.pallas_call(
        kernel,
        name="titans",
        out_shape=jax.ShapeDtypeStruct((T, W), BF16),
        in_specs=[vm] * 9 + [sm] + [vm] * 5,
        out_specs=vm,
        scratch_shapes=[
            big, big, big, big, big,
            V((1024, W), BF16), V((T, W), BF16), V((T, W), BF16), V((T, W), BF16), V((T, W), BF16), V((T, W), BF16),
            V((T, W), BF16), V((T, W), F32), V((T, W), BF16), V((1024, W), BF16), V((W, 1024), BF16), V((1024, W), F32),
            V((64, W), F32), V((64, W), F32), V((1024, T), BF16),
            V((2, 7, T, W), BF16), V((2, 7, T, W), BF16), V((NS, 8, W), F32), V((8, W), F32),
            slab, slab, slab, slab,
            V((9, T, 2 * W), BF16), V((4, 256, W), BF16), big, V((4, 256, 1), F32), V((4, 256, 2 * W), F32),
            dma((4, PARTS, 6)), dma((4, PARTS, 6)), dma((7,)), dma((7,)), dma((2, 7)), dma((2, 7)), dma((21,)), dma((21,)),
            dma((7,)), dma((7,)), dma, dma,
            dma, dma((NS,)), dma, dma, dma((10,)), dma((9,)),
        ],
        compiler_params=pltpu.CompilerParams(collective_id=0, has_side_effects=True, vmem_limit_bytes=60 * 1024 * 1024),
    )(
        tokens, mem_query_w, mem_key_w, mem_value_w, mem_in, mem_out, forget_levels, momentum_levels, step_levels,
        plan, norm_gain.reshape(1, -1), attn_query_w, attn_key_w, attn_value_w, attn_out_w,
    )


def solution(mesh):
    seq, head = P("seq", None), P(None, "head")
    in_specs = (
        seq, head, head, head, head, P("head", None), head, head, head, P("seq"), P(), head, head, head, P("head", None),
    )
    return jax.shard_map(block, mesh=mesh, in_specs=in_specs, out_specs=P("seq", "head"), check_vma=False)
```

time: 177 us -> 157 us (0.89)
  Pallas kernels: 174 us -> 153 us
    pallas_call x1, Pallas kernels: 174 us -> 153 us  [block(): pl.pallas_call(kernel, name='titans', out_shape=jax.ShapeDtypeStruct((T,...]
where the time goes in v3:
time: 157 us; the launch traced here: 156 us
  Pallas kernels  153 us (97%)
  local copies, waits for them, and re-layouts  1.57 us (1%)
    pallas_call x1, Pallas kernels, block(): pl.pallas_call(kernel, name='titans', out_shape=jax.ShapeDtypeStruct((T,...  153 us

profile of v3, /device:TPU:6, one launch (start us, length us, event | category | flops | bytes accessed | tf_op | source)
XLA Modules:
  0.0 155.7 jit_solution(12360194120836652740)
XLA Ops:
  0.7 153.5 %titans.1 = bf16[512,128]{1,0:T(8,128)(2,1)} custom-call(bf16[512,1024]{1,0:T(8,128)(2,1)} %tok.1, bf16[1024,128]{1,0:T(8,128)(2,1)} %wq.1, bf16[1024,128]{1,0:T(8,128)(2,1)} %wk.1, bf16[1024,128]{1,0:T(8,128)(2,1)} %wv.1, f32[1024,128]{1,0:T(8,128)} %m_in.1, f32[128,1024]{1,0:T(8,128)} %m_out.1, f32[16,128]{1,0:T(8,128)} %fg.1, f32[16,128]{1,0:T(8,128)} %mo.1, ...), custom_call_target="tpu_custom_call" | custom-call | tf_op jit(solution)/shard_map/titans/pallas_call | solution.py:641
  154.1 1.6 %copy.18 = bf16[512,128]{1,0:T(8,128)(2,1)} copy(bf16[512,128]{1,0:T(8,128)(2,1)} %titans.1) | data formatting | bytes 262144

commit v4 on v3

--- a/solution.py
+++ b/solution.py
@@ -92,80 +92,97 @@
         return (self.s + 1 - 2 * self.k, self.y * 2 + self.z)
 
 
-def gather(core, buf, send, recv):
-    me, k = core, core.k
-
-    def copy(n, y, to):
-        ref = buf.at[:, col(y * 2 + k)]
-        return remote(ref, ref, send.at[n], recv.at[n], to)
-
-    c = (
-        copy(0, me.y, me.at(me.next)),
-        copy(1, me.y, me.at(me.prev)),
-        copy(2, me.prev, me.at(me.next)),
-        copy(3, me.y, me.other()),
-        copy(4, me.prev, me.other()),
-        copy(5, me.next, me.other()),
-        copy(6, me.far, me.other()),
-    )
-
-    def start():
+class Share:
+    def __init__(self, core, buf, send, recv):
+        self.me, self.buf, self.send, self.recv = core, buf, send, recv
+
+    def copy(self, c, n):
+        me = self.me
+        y = (me.y, me.y, me.prev, me.y, me.prev, me.next, me.far)[n]
+        to = (me.at(me.next), me.at(me.prev), me.at(me.next), me.other(), me.other(), me.other(), me.other())[n]
+        ref = self.buf.at[half(c), col(y * 2 + me.k)]
+        return remote(ref, ref, self.send.at[c, n], self.recv.at[c, n], to)
+
+    def start(self, c):
         for n in (0, 1, 3):
-            c[n].start()
-
-    def finish():
-        c[0].wait_recv()
-        c[2].start()
-        c[4].start()
-        c[1].wait_recv()
-        c[5].start()
-        c[2].wait_recv()
-        c[6].start()
+            self.copy(c, n).start()
+
+    def step(self, c):
+        self.copy(c, 0).wait_recv()
+        self.copy(c, 2).start()
+        self.copy(c, 4).start()
+        self.copy(c, 1).wait_recv()
+        self.copy(c, 5).start()
+
+    def last(self, c):
+        self.copy(c, 2).wait_recv()
+        self.copy(c, 6).start()
+
+    def finish(self, c):
         for n in (3, 4, 5, 6):
-            c[n].wait_recv()
-
-    return start, finish, c
-
-
-def reduce_scatter(core, part, out, land, send, recv):
-    me, k = core, core.k
-
-    def copy(n, to):
-        return remote(out.at[n], land.at[n], send.at[n], recv.at[n], to)
-
-    order = (me.far, me.next, me.prev, me.y)
-    c = tuple(copy(n, me.other()) for n in range(4)) + (copy(4, me.at(me.next)), copy(5, me.at(me.next)), copy(6, me.at(me.prev)))
-    slot = (0, 2, 1, 3)
-    for n, y in enumerate(order):
-        out[n] = part(y * 2 + 1 - k).astype(BF16)
-        c[n].start()
-
-    def chip(n):
-        mine = part(order[n] * 2 + k)
-        c[slot[n]].wait_recv()
-        return mine + land[slot[n]].astype(F32)
-
-    out[4] = chip(0).astype(BF16)
-    c[4].start()
-    out[6] = chip(2).astype(BF16)
-    c[6].start()
-    onward = chip(1)
-    own = chip(3)
-    c[4].wait_recv()
-    out[5] = (land[4].astype(F32) + onward).astype(BF16)
-    c[5].start()
-    c[6].wait_recv()
-    own = own + land[6].astype(F32)
-    c[5].wait_recv()
-    return own + land[5].astype(F32), c
+            self.copy(c, n).wait_recv()
+
+    def drain(self):
+        for c in range(PARTS):
+            for n in range(7):
+                self.copy(c, n).wait_send()
+
+
+class Sum:
+    def __init__(self, core, part, out, land, send, recv):
+        self.me, self.part, self.out, self.land, self.send, self.recv = core, part, out, land, send, recv
+        self.order = (core.far, core.next, core.prev, core.y)
+
+    def copy(self, c, n):
+        me = self.me
+        to = me.other() if n < 4 else me.at(me.prev if n == 6 else me.next)
+        return remote(self.out.at[n, half(c)], self.land.at[n, half(c)], self.send.at[c, n], self.recv.at[c, n], to)
+
+    def put(self, c, n, value):
+        self.out[n, half(c), :] = value.astype(BF16)
+        self.copy(c, n).start()
+
+    def got(self, c, n):
+        self.copy(c, n).wait_recv()
+        return self.land[n, half(c), :].astype(F32)
+
+    def give(self, c):
+        for n, y in enumerate(self.order):
+            self.put(c, n, self.part(c, y * 2 + 1 - self.me.k))
+
+    def chip(self, c, n):
+        return self.part(c, self.order[n] * 2 + self.me.k) + self.got(c, (0, 2, 1, 3)[n])
+
+    def first(self, c):
+        self.put(c, 4, self.chip(c, 0))
+        self.put(c, 6, self.chip(c, 2))
+
+    def second(self, c):
+        onward = self.chip(c, 1)
+        self.put(c, 5, self.got(c, 4) + onward)
+
+    def last(self, c):
+        own = self.chip(c, 3)
+        return own + self.got(c, 6) + self.got(c, 5)
+
+    def run(self):
+        for stage in (self.give, self.first, self.second):
+            for c in range(PARTS):
+                stage(c)
+
+    def drain(self):
+        for c in range(PARTS):
+            for n in range(7):
+                self.copy(c, n).wait_send()
 
 
 def kernel(
-    tok, wq, wk, wv, m_in, m_out, fg, mo, st, plan, gain, aq, ak, av, ao, out_ref,
+    tok_h, wq_h, wk_h, wv_h, m_in_h, m_out_h, fg, mo, st, plan, gain, aq_h, ak_h, av_h, ao_h, out_ref,
+    tok, wk, wq, wv, m_in, m_out, aq, ak, av, ao, l_sem,
     kf, qf, rf, tf, cf, wo, kb, qb, vb, tb, vbuf, hid, slope, hq, mi, mob, mot, w0, w0s, kt,
     rs_out, rs_land, gates, gown, gbuf, rbuf, wbuf, wland, kv, qs, nrm, m_s, acc,
     g_send, g_recv, h_send, h_recv, r_send, r_recv, p_send, p_recv, w_send, w_recv, gt_send, gt_recv,
-    a_send, a_recv, b_send, b_recv, k_send, k_recv,
+    a_send, a_recv, b_send, b_recv, k_send, k_recv, x_send, x_recv,
 ):
     s, h = lax.axis_index("seq"), lax.axis_index("head")
     y, z = h // 2, h % 2
@@ -200,6 +217,14 @@
     for to in (aside, pair):
         pl.semaphore_signal(barrier, inc=1, device_id=to, device_id_type=MESH)
 
+    pairs = (
+        (tok_h, tok), (wk_h, wk), (m_in_h, m_in), (m_out_h, m_out), (wq_h, wq), (wv_h, wv), (ao_h, ao), (ak_h, ak), (av_h, av), (aq_h, aq),
+    )
+    loads = [pltpu.make_async_copy(src, dst, l_sem.at[n]) for n, (src, dst) in enumerate(pairs)]
+    for load in loads:
+        load.start()
+    loads[0].wait()
+    loads[1].wait()
     key = dot(tok[...], wk[...]).astype(BF16)
     kb[...] = key
 
@@ -215,11 +240,15 @@
     gown[...] = jnp.concatenate([row(mo), 1.0 - row(fg), row(st), jnp.zeros((5, W), F32)], axis=0)
     pl.semaphore_wait(barrier, NH - 1 + NS - 1 + 2)
 
+    for load in loads[2:]:
+        load.wait()
     ring_k = Ring(place, z, kf, g_send.at[0], g_recv.at[0])
     ring_q = Ring(place, z, qf, g_send.at[1], g_recv.at[1])
     ring_t = Ring(place, par, tf, g_send.at[2], g_recv.at[2])
     ring_c = Ring(place, z, cf, g_send.at[3], g_recv.at[3])
 
+    x = s // 8
+
     def z_copy(n, c, src, dst):
         return send(n + c, src.at[half(c)], dst.at[half(c), col(h)], across)
 
@@ -233,10 +262,19 @@
         return send(5, gown, gates.at[s], pair)
 
     def mi_copy():
-        return send(6, mi, mi, across)
+        ref = mi.at[pl.ds(pl.multiple_of(x * 256, 256), 256), :]
+        return send(6, ref, ref, across)
 
     def mo_copy():
-        return send(7, mob, mob, across)
+        ref = mob.at[pl.ds(pl.multiple_of(x * 32, 32), 32), :]
+        return send(7, ref, ref, across)
+
+    def share_copy(d, n):
+        if n == 0:
+            ref = mi.at[pl.ds(pl.multiple_of(x * 256, 256), 256), :]
+        else:
+            ref = mob.at[pl.ds(pl.multiple_of(x * 32, 32), 32), :]
+        return remote(ref, ref, x_send.at[n, d - 1], x_recv.at[n, d - 1], ((x + d) % 4 * 8 + s % 8, h))
 
     def w0_copy():
         return send(8, w0s, w0, across)
@@ -293,8 +331,13 @@
 
     @pl.when(away)
     def _():
-        mi_copy().wait_recv()
-        mo_copy().wait_recv()
+        for n, copy in enumerate((mi_copy, mo_copy)):
+            copy().wait_recv()
+            for d in (2, 1, 3):
+                share_copy(d, n).start()
+        for n in range(2):
+            for d in (1, 2, 3):
+                share_copy(d, n).wait_recv()
         for c in range(PARTS):
             side_rows(9, c, kf).wait_recv()
         for c in range(PARTS):
@@ -305,10 +348,11 @@
     hid[...] = (pre * sig).astype(BF16)
     slope[...] = sig * (1.0 + pre * (1.0 - sig))
 
-    def part_one(b):
-        return dot(hid[...], mob[:, col(b)])
-
-    predicted, sent_one = reduce_scatter(core, part_one, rs_out.at[0], rs_land.at[0], r_send.at[0], r_recv.at[0])
+    def part_one(c, b):
+        return dot(hid[half(c), :], mob[:, col(b)])
+
+    sum_one = Sum(core, part_one, rs_out.at[0], rs_land.at[0], r_send.at[0], r_recv.at[0])
+    sum_one.run()
 
     @pl.when(away)
     def _():
@@ -317,9 +361,10 @@
         w0_copy().wait_recv()
 
     own = core.y * 2 + par
-    rf[:, col(own)] = ((2.0 / T) * (predicted - vbuf[...].astype(F32))).astype(BF16)
-    r_start, r_finish, sent_r = gather(core, rf, h_send, h_recv)
-    r_start()
+    share_r = Share(core, rf, h_send, h_recv)
+    for c in range(PARTS):
+        rf[half(c), col(own)] = ((2.0 / T) * (sum_one.last(c) - vbuf[half(c), :].astype(F32))).astype(BF16)
+        share_r.start(c)
 
     def send_gates(d, carry):
         remote(gates.at[g], gates.at[g], gt_send, gt_recv, group((g + d) % NS)).start()
@@ -327,7 +372,9 @@
 
     lax.fori_loop(1, NS, send_gates, 0)
     kt[...] = kf[...].T
-    r_finish()
+    for stage in (share_r.step, share_r.last, share_r.finish):
+        for c in range(PARTS):
+            stage(c)
 
     @pl.when(home)
     def _():
@@ -406,32 +453,38 @@
     act = dot(qf[...], wland[:, 0:32, :].reshape(1024, W))
     hq[...] = (act * jax.nn.sigmoid(act)).astype(BF16)
 
-    def part_two(b):
-        return dot(hq[...], wland[pl.ds(b * 4, 4), 32:64, :].reshape(W, W), NT)
-
-    retrieved, sent_two = reduce_scatter(core, part_two, rs_out.at[1], rs_land.at[1], r_send.at[1], r_recv.at[1])
-
-    tb[...] = retrieved.astype(BF16)
+    def part_two(c, b):
+        return dot(hq[half(c), :], wland[pl.ds(b * 4, 4), 32:64, :].reshape(W, W), NT)
+
+    sum_two = Sum(core, part_two, rs_out.at[1], rs_land.at[1], r_send.at[1], r_recv.at[1])
+    sum_two.run()
 
     def t_copy(n, c, to):
         return send(n + c, tb.at[half(c)], tf.at[half(c), col(own)], to)
 
-    @pl.when(home)
-    def _():
-        for c in range(PARTS):
+    for c in range(PARTS):
+        rows_c = sum_two.last(c).astype(BF16)
+        tb[half(c), :] = rows_c
+
+        @pl.when(home)
+        def _():
             t_copy(13, c, across).start()
-        tf[:, col(own)] = tb[...]
-        for c in range(PARTS):
+            tf[half(c), col(own)] = rows_c
             ring_t.give_a(c)
+
+        @pl.when(away)
+        def _():
+            t_copy(15, c, pair).start()
+            t_copy(17, c, aside).start()
+
+    @pl.when(home)
+    def _():
         for c in range(PARTS):
             t_copy(17, c, aside).wait_recv()
             ring_t.give_b(c)
 
     @pl.when(away)
     def _():
-        for c in range(PARTS):
-            t_copy(17, c, aside).start()
-            t_copy(15, c, pair).start()
         for c in range(PARTS):
             t_copy(13, c, across).wait_recv()
             ring_t.give_a(c)
@@ -440,31 +493,22 @@
 
     for c in range(PARTS):
         ring_t.relay(c)
-    for c in range(PARTS):
-        ring_t.finish(c)
-    for i in range(4):
-        r = slice(i * 128, (i + 1) * 128)
-        x = tf[r, :].astype(F32)
-        mean = jnp.mean(x * x, axis=-1, keepdims=True)
-        nrm[r, :] = (x * lax.rsqrt(mean + EPS) * gain[...]).astype(BF16)
-    kv[0, :, 0:W] = dot(nrm[...], ak[...]).astype(BF16)
-    kv[0, :, W : 2 * W] = dot(nrm[...], av[...]).astype(BF16)
-
     zl = (s // 2) % 4
 
-    def own_copy(k):
-        return remote(kv.at[0], kv.at[2 * k], k_send.at[k], k_recv.at[2 * k], (s + 2 * k, h))
-
-    def side_copy():
-        return remote(kv.at[0], kv.at[1], k_send.at[0], k_recv.at[1], (s + 1, h))
-
-    def pass_copy(k):
-        to = 2 * k + 1 - 2 * par
-        return remote(kv.at[2 * k], kv.at[to], k_send.at[4 + k], k_recv.at[to], (s + 1 - 2 * par, h))
-
-    def relay_copy(up):
-        to = 6 if up else 2
-        return remote(kv.at[4], kv.at[to], k_send.at[9], k_recv.at[to], (s + 2 if up else s - 2, h))
+    def hop(c, n, slot, to_slot, to):
+        return remote(kv.at[slot, half(c)], kv.at[to_slot, half(c)], k_send.at[c, n], k_recv.at[c, to_slot], to)
+
+    def own_copy(c, k):
+        return hop(c, k, 0, 2 * k, (s + 2 * k, h))
+
+    def side_copy(c):
+        return hop(c, 0, 0, 1, (s + 1, h))
+
+    def pass_copy(c, k):
+        return hop(c, 4 + k, 2 * k, 2 * k + 1 - 2 * par, (s + 1 - 2 * par, h))
+
+    def relay_copy(c, up):
+        return hop(c, 9, 4, 6 if up else 2, (s + 2 if up else s - 2, h))
 
     def sends(k):
         ok = s + 2 * k < NS
@@ -477,15 +521,24 @@
     def passes(k):
         return (s >= 2 * k) & ((par == 1) | (k < 4))
 
-    for k in (2, 1, 3, 4):
-
-        @pl.when(sends(k))
-        def _():
-            own_copy(k).start()
-
-    @pl.when(par == 0)
-    def _():
-        side_copy().start()
+    for c in range(PARTS):
+        ring_t.finish(c)
+        for i in range(2):
+            r = slice(c * HALF + i * 128, c * HALF + (i + 1) * 128)
+            rows_i = tf[r, :].astype(F32)
+            mean = jnp.mean(rows_i * rows_i, axis=-1, keepdims=True)
+            nrm[r, :] = (rows_i * lax.rsqrt(mean + EPS) * gain[...]).astype(BF16)
+        kv[0, half(c), 0:W] = dot(nrm[half(c), :], ak[...]).astype(BF16)
+        kv[0, half(c), W : 2 * W] = dot(nrm[half(c), :], av[...]).astype(BF16)
+        for k in (2, 1, 3, 4):
+
+            @pl.when(sends(k))
+            def _():
+                own_copy(c, k).start()
+
+        @pl.when(par == 0)
+        def _():
+            side_copy(c).start()
 
     query = dot(nrm[...], aq[...]).astype(BF16) * 0.125
     low = lax.broadcasted_iota(jnp.int32, (128, W), 1) < 64
@@ -512,8 +565,8 @@
             acc[i] = jnp.exp(m_old - m_new) * acc[i] + dot(p.astype(BF16), values)
 
     attend(0, 0)
-    def arrive(slot):
-        remote(kv.at[0], kv.at[slot], k_send.at[0], k_recv.at[slot], (s, h ^ 1)).wait_recv()
+    def arrive(c, slot):
+        hop(c, 0, 0, slot, across).wait_recv()
 
     last = jnp.where(zl == 0, 1, 3)
 
@@ -526,25 +579,27 @@
 
         @pl.when((j < 4) & (s >= 2 * k))
         def _():
-            arrive(2 * k)
-
-            @pl.when((k == 2) & (zl == 2))
-            def _():
-                relay_copy(True).start()
-
-            @pl.when((k == 2) & (zl == 1))
-            def _():
-                relay_copy(False).start()
-
-            @pl.when(passes(k))
-            def _():
-                pass_copy(k).start()
+            for c in range(PARTS):
+                arrive(c, 2 * k)
+
+                @pl.when((k == 2) & (zl == 2))
+                def _():
+                    relay_copy(c, True).start()
+
+                @pl.when((k == 2) & (zl == 1))
+                def _():
+                    relay_copy(c, False).start()
+
+                @pl.when(passes(k))
+                def _():
+                    pass_copy(c, k).start()
 
             attend(2 * k, 2, jnp.where(k == 4, 0, -2 * T))
 
         @pl.when((odd > 0) & (odd < 9) & (s >= odd))
         def _():
-            arrive(odd)
+            for c in range(PARTS):
+                arrive(c, odd)
             attend(odd, 1)
 
         return carry
@@ -593,39 +648,43 @@
             t_copy(15, c, pair).wait_send()
         v_copy().wait_send()
         gate_copy().wait_send()
+        for n in range(2):
+            for d in (1, 2, 3):
+                share_copy(d, n).wait_send()
 
     ring_t.drain()
     ring_c.drain()
     for c in range(PARTS):
         c_copy(c).wait_send()
-    for c in sent_one + sent_two + sent_r:
-        c.wait_send()
+    for group_copies in (sum_one, sum_two, share_r):
+        group_copies.drain()
     for d in range(1, NH):
         wo_copy(d).wait_send()
     pltpu.make_async_copy(gates.at[some], gates.at[some], gt_send).wait()
     pltpu.make_async_copy(gbuf.at[some], gbuf.at[some], a_send).wait()
     pltpu.make_async_copy(wbuf.at[some], wbuf.at[some], b_send).wait()
-    for k in range(1, 5):
-
-        @pl.when(sends(k))
-        def _():
-            own_copy(k).wait_send()
-
-        @pl.when(passes(k))
-        def _():
-            pass_copy(k).wait_send()
-
-    @pl.when(par == 0)
-    def _():
-        side_copy().wait_send()
-
-    @pl.when((s >= 4) & (zl == 2))
-    def _():
-        relay_copy(True).wait_send()
-
-    @pl.when((s >= 4) & (zl == 1))
-    def _():
-        relay_copy(False).wait_send()
+    for c in range(PARTS):
+        for k in range(1, 5):
+
+            @pl.when(sends(k))
+            def _():
+                own_copy(c, k).wait_send()
+
+            @pl.when(passes(k))
+            def _():
+                pass_copy(c, k).wait_send()
+
+        @pl.when(par == 0)
+        def _():
+            side_copy(c).wait_send()
+
+        @pl.when((s >= 4) & (zl == 2))
+        def _():
+            relay_copy(c, True).wait_send()
+
+        @pl.when((s >= 4) & (zl == 1))
+        def _():
+            relay_copy(c, False).wait_send()
 
 
 def block(
@@ -634,6 +693,7 @@
 ):
     vm = pl.BlockSpec(memory_space=pltpu.VMEM)
     sm = pl.BlockSpec(memory_space=pltpu.SMEM)
+    hb = pl.BlockSpec(memory_space=pl.ANY)
     V = pltpu.VMEM
     dma = pltpu.SemaphoreType.DMA
     big = V((T, 1024), BF16)
@@ -642,9 +702,11 @@
         kernel,
         name="titans",
         out_shape=jax.ShapeDtypeStruct((T, W), BF16),
-        in_specs=[vm] * 9 + [sm] + [vm] * 5,
+        in_specs=[hb] * 6 + [vm] * 3 + [sm, vm] + [hb] * 4,
         out_specs=vm,
         scratch_shapes=[
+            big, V((1024, W), BF16), V((1024, W), BF16), V((1024, W), BF16), V((1024, W), F32), V((W, 1024), F32),
+            V((1024, W), BF16), V((1024, W), BF16), V((1024, W), BF16), V((W, 1024), BF16), dma((10,)),
             big, big, big, big, big,
             V((1024, W), BF16), V((T, W), BF16), V((T, W), BF16), V((T, W), BF16), V((T, W), BF16), V((T, W), BF16),
             V((T, W), BF16), V((T, W), F32), V((T, W), BF16), V((1024, W), BF16), V((W, 1024), BF16), V((1024, W), F32),
@@ -652,9 +714,9 @@
             V((2, 7, T, W), BF16), V((2, 7, T, W), BF16), V((NS, 8, W), F32), V((8, W), F32),
             slab, slab, slab, slab,
             V((9, T, 2 * W), BF16), V((4, 256, W), BF16), big, V((4, 256, 1), F32), V((4, 256, 2 * W), F32),
-            dma((4, PARTS, 6)), dma((4, PARTS, 6)), dma((7,)), dma((7,)), dma((2, 7)), dma((2, 7)), dma((21,)), dma((21,)),
+            dma((4, PARTS, 6)), dma((4, PARTS, 6)), dma((PARTS, 7)), dma((PARTS, 7)), dma((2, PARTS, 7)), dma((2, PARTS, 7)), dma((21,)), dma((21,)),
             dma((7,)), dma((7,)), dma, dma,
-            dma, dma((NS,)), dma, dma, dma((10,)), dma((9,)),
+            dma, dma((NS,)), dma, dma, dma((PARTS, 10)), dma((PARTS, 9)), dma((2, 3)), dma((2, 3)),
         ],
         compiler_params=pltpu.CompilerParams(collective_id=0, has_side_effects=True, vmem_limit_bytes=60 * 1024 * 1024),
     )(

time: 157 us -> 149 us (0.949)
  Pallas kernels: 153 us -> 146 us
    pallas_call x1, Pallas kernels: 153 us -> 146 us  [block(): pl.pallas_call(kernel, name='titans', out_shape=jax.ShapeDtypeStruct((T,...]
where the time goes in v4:
time: 149 us
  Pallas kernels  146 us (98%)
  local copies, waits for them, and re-layouts  1.57 us (1%)
    pallas_call x1, Pallas kernels, block(): pl.pallas_call(kernel, name='titans', out_shape=jax.ShapeDtypeStruct((T,...  146 us

profile of v4, /device:TPU:6, one launch (start us, length us, event | category | flops | bytes accessed | tf_op | source)
XLA Modules:
  0.0 148.7 jit_solution(6455494985721002068)
XLA Ops:
  0.7 146.5 %titans.1 = bf16[512,128]{1,0:T(8,128)(2,1)} custom-call(bf16[512,1024]{1,0:T(8,128)(2,1)} %tok_h.1, bf16[1024,128]{1,0:T(8,128)(2,1)} %wq_h.1, bf16[1024,128]{1,0:T(8,128)(2,1)} %wk_h.1, bf16[1024,128]{1,0:T(8,128)(2,1)} %wv_h.1, f32[1024,128]{1,0:T(8,128)} %m_in_h.1, f32[128,1024]{1,0:T(8,128)} %m_out_h.1, f32[16,128]{1,0:T(8,128)} %fg.1, f32[16,128]{1,0:T(8,128)} %mo.1, ...), custom_call_target="tpu_custom_call" | custom-call | tf_op jit(solution)/shard_map/titans/pallas_call | solution.py:701
  147.1 1.6 %copy.18 = bf16[512,128]{1,0:T(8,128)(2,1)} copy(bf16[512,128]{1,0:T(8,128)(2,1)} %titans.1) | data formatting | bytes 262144

commit v5 on v4

--- a/solution.py
+++ b/solution.py
@@ -31,12 +31,17 @@
     )
 
 
-HALF = T // 2
-PARTS = 2
+WINS = 2
+PARTS = 4
+HALF = T // PARTS
 
 
 def half(c):
     return pl.ds(c * HALF, HALF)
+
+
+def wait(ref, sem):
+    pltpu.make_async_copy(ref, ref, sem).wait()
 
 
 class Ring:
@@ -50,7 +55,7 @@
         up, down = (y + 1) % 4, (y + 3) % 4
         block, to = ((y * 2 + a, up), (y * 2 + a, down), (y * 2 + b, up), (y * 2 + b, down), (down * 2 + a, up), (up * 2 + b, down))[k]
         ref = self.buf.at[half(c), col(block)]
-        return remote(ref, ref, self.send.at[c, k], self.recv.at[c, k], (self.s, to * 2 + self.z))
+        return remote(ref, ref, self.send, self.recv.at[c, (0, 2, 2, 1, 2, 2)[k]], (self.s, to * 2 + self.z))
 
     def give_a(self, c):
         self.copy(c, 0).start()
@@ -67,13 +72,10 @@
         self.copy(c, 5).start()
 
     def finish(self, c):
-        for k in (1, 2, 4, 5):
-            self.copy(c, k).wait_recv()
+        wait(self.buf.at[half(c), pl.ds(0, 4 * W)], self.recv.at[c, 2])
 
     def drain(self):
-        for c in range(PARTS):
-            for k in range(6):
-                self.copy(c, k).wait_send()
+        wait(self.buf.at[pl.ds(0, T * 6 // 8)], self.send)
 
 
 class Core:
@@ -101,7 +103,7 @@
         y = (me.y, me.y, me.prev, me.y, me.prev, me.next, me.far)[n]
         to = (me.at(me.next), me.at(me.prev), me.at(me.next), me.other(), me.other(), me.other(), me.other())[n]
         ref = self.buf.at[half(c), col(y * 2 + me.k)]
-        return remote(ref, ref, self.send.at[c, n], self.recv.at[c, n], to)
+        return remote(ref, ref, self.send, self.recv.at[c, min(n, 3)], to)
 
     def start(self, c):
         for n in (0, 1, 3):
@@ -119,13 +121,10 @@
         self.copy(c, 6).start()
 
     def finish(self, c):
-        for n in (3, 4, 5, 6):
-            self.copy(c, n).wait_recv()
+        wait(self.buf.at[half(c), pl.ds(0, 4 * W)], self.recv.at[c, 3])
 
     def drain(self):
-        for c in range(PARTS):
-            for n in range(7):
-                self.copy(c, n).wait_send()
+        wait(self.buf.at[pl.ds(0, T * 7 // 8)], self.send)
 
 
 class Sum:
@@ -136,7 +135,7 @@
     def copy(self, c, n):
         me = self.me
         to = me.other() if n < 4 else me.at(me.prev if n == 6 else me.next)
-        return remote(self.out.at[n, half(c)], self.land.at[n, half(c)], self.send.at[c, n], self.recv.at[c, n], to)
+        return remote(self.out.at[n, half(c)], self.land.at[n, half(c)], self.send, self.recv.at[c, max(n - 3, 0)], to)
 
     def put(self, c, n, value):
         self.out[n, half(c), :] = value.astype(BF16)
@@ -151,9 +150,10 @@
             self.put(c, n, self.part(c, y * 2 + 1 - self.me.k))
 
     def chip(self, c, n):
-        return self.part(c, self.order[n] * 2 + self.me.k) + self.got(c, (0, 2, 1, 3)[n])
+        return self.part(c, self.order[n] * 2 + self.me.k) + self.land[(0, 2, 1, 3)[n], half(c), :].astype(F32)
 
     def first(self, c):
+        wait(self.land.at[pl.ds(0, 4), half(c)], self.recv.at[c, 0])
         self.put(c, 4, self.chip(c, 0))
         self.put(c, 6, self.chip(c, 2))
 
@@ -171,17 +171,15 @@
                 stage(c)
 
     def drain(self):
-        for c in range(PARTS):
-            for n in range(7):
-                self.copy(c, n).wait_send()
+        wait(self.out, self.send)
 
 
 def kernel(
     tok_h, wq_h, wk_h, wv_h, m_in_h, m_out_h, fg, mo, st, plan, gain, aq_h, ak_h, av_h, ao_h, out_ref,
-    tok, wk, wq, wv, m_in, m_out, aq, ak, av, ao, l_sem,
+    tok, wk, wq, wv, m_in, m_out, aq, ak, av, ao, l_sem, ob, o_sem,
     kf, qf, rf, tf, cf, wo, kb, qb, vb, tb, vbuf, hid, slope, hq, mi, mob, mot, w0, w0s, kt,
     rs_out, rs_land, gates, gown, gbuf, rbuf, wbuf, wland, kv, qs, nrm, m_s, acc,
-    g_send, g_recv, h_send, h_recv, r_send, r_recv, p_send, p_recv, w_send, w_recv, gt_send, gt_recv,
+    g_send, g_recv, h_send, h_recv, r_send, r_recv, p_send, p_recv, q_recv, w_send, w_recv, gt_send, gt_recv,
     a_send, a_recv, b_send, b_recv, k_send, k_recv, x_send, x_recv,
 ):
     s, h = lax.axis_index("seq"), lax.axis_index("head")
@@ -199,8 +197,8 @@
     def group(c):
         return (c // 2 * 2 + par, y * 2 + c % 2)
 
-    def send(n, src, dst, to):
-        return remote(src, dst, p_send.at[n], p_recv.at[n], to)
+    def send(n, src, dst, to, c=0):
+        return remote(src, dst, p_send.at[n], p_recv.at[n * PARTS + c] if n < 6 else q_recv.at[n - 6], to)
 
     barrier = pltpu.get_barrier_semaphore()
 
@@ -250,34 +248,34 @@
     x = s // 8
 
     def z_copy(n, c, src, dst):
-        return send(n + c, src.at[half(c)], dst.at[half(c), col(h)], across)
+        return send(n, src.at[half(c)], dst.at[half(c), col(h)], across, c)
 
     def side_rows(n, c, buf):
-        return send(n + c, buf.at[half(c)], buf.at[half(c)], aside)
+        return send(n, buf.at[half(c)], buf.at[half(c)], aside, c)
 
     def v_copy():
-        return send(4, vb, vbuf, pair)
+        return send(8, vb, vbuf, pair)
 
     def gate_copy():
-        return send(5, gown, gates.at[s], pair)
+        return send(9, gown, gates.at[s], pair)
 
     def mi_copy():
         ref = mi.at[pl.ds(pl.multiple_of(x * 256, 256), 256), :]
-        return send(6, ref, ref, across)
+        return send(10, ref, ref, across)
 
     def mo_copy():
         ref = mob.at[pl.ds(pl.multiple_of(x * 32, 32), 32), :]
-        return send(7, ref, ref, across)
+        return send(11, ref, ref, across)
 
     def share_copy(d, n):
         if n == 0:
             ref = mi.at[pl.ds(pl.multiple_of(x * 256, 256), 256), :]
         else:
             ref = mob.at[pl.ds(pl.multiple_of(x * 32, 32), 32), :]
-        return remote(ref, ref, x_send.at[n, d - 1], x_recv.at[n, d - 1], ((x + d) % 4 * 8 + s % 8, h))
+        return remote(ref, ref, x_send, x_recv.at[n], ((x + d) % 4 * 8 + s % 8, h))
 
     def w0_copy():
-        return send(8, w0s, w0, across)
+        return send(12, w0s, w0, across)
 
     @pl.when(home)
     def _():
@@ -327,7 +325,7 @@
             ring_k.relay(c)
         for c in range(PARTS):
             ring_k.finish(c)
-            side_rows(9, c, kf).start()
+            side_rows(1, c, kf).start()
 
     @pl.when(away)
     def _():
@@ -335,13 +333,12 @@
             copy().wait_recv()
             for d in (2, 1, 3):
                 share_copy(d, n).start()
-        for n in range(2):
-            for d in (1, 2, 3):
-                share_copy(d, n).wait_recv()
-        for c in range(PARTS):
-            side_rows(9, c, kf).wait_recv()
-        for c in range(PARTS):
-            z_copy(2, c, qb, qf).start()
+        wait(mi.at[pl.ds(0, 768)], x_recv.at[0])
+        wait(mob.at[pl.ds(0, 96)], x_recv.at[1])
+        for c in range(PARTS):
+            side_rows(1, c, kf).wait_recv()
+        for c in range(PARTS):
+            z_copy(6, c, qb, qf).start()
 
     pre = dot(kf[...], mi[...])
     sig = jax.nn.sigmoid(pre)
@@ -397,7 +394,7 @@
 
     def wo_copy(d):
         p = (h + d) % NH
-        return remote(ao.at[:, col(p)], wo.at[pl.ds(pl.multiple_of(h * W, W), W), :], w_send.at[d - 1], w_recv.at[d - 1], (s, p))
+        return remote(ao.at[:, col(p)], wo.at[pl.ds(pl.multiple_of(h * W, W), W), :], w_send, w_recv, (s, p))
 
     for d in range(1, NH):
         wo_copy(d).start()
@@ -423,8 +420,8 @@
 
     @pl.when(home)
     def _():
-        for c in range(PARTS):
-            z_copy(2, c, qb, qf).wait_recv()
+        wait(qb, q_recv.at[0])
+        for c in range(PARTS):
             ring_q.give_b(c)
 
     state = lax.fori_loop(4, 20, step, state)
@@ -440,12 +437,11 @@
     def _():
         for c in range(PARTS):
             ring_q.finish(c)
-            side_rows(11, c, qf).start()
+            side_rows(7, c, qf).start()
 
     @pl.when(away)
     def _():
-        for c in range(PARTS):
-            side_rows(11, c, qf).wait_recv()
+        wait(qf, q_recv.at[1])
 
     some = pl.ds(0, NS - 1)
     pltpu.make_async_copy(wland.at[some], wland.at[some], b_recv).wait()
@@ -460,7 +456,7 @@
     sum_two.run()
 
     def t_copy(n, c, to):
-        return send(n + c, tb.at[half(c)], tf.at[half(c), col(own)], to)
+        return send(n, tb.at[half(c)], tf.at[half(c), col(own)], to, c)
 
     for c in range(PARTS):
         rows_c = sum_two.last(c).astype(BF16)
@@ -468,27 +464,27 @@
 
         @pl.when(home)
         def _():
-            t_copy(13, c, across).start()
+            t_copy(2, c, across).start()
             tf[half(c), col(own)] = rows_c
             ring_t.give_a(c)
 
         @pl.when(away)
         def _():
-            t_copy(15, c, pair).start()
-            t_copy(17, c, aside).start()
-
-    @pl.when(home)
-    def _():
-        for c in range(PARTS):
-            t_copy(17, c, aside).wait_recv()
+            t_copy(3, c, pair).start()
+            t_copy(4, c, aside).start()
+
+    @pl.when(home)
+    def _():
+        for c in range(PARTS):
+            t_copy(4, c, aside).wait_recv()
             ring_t.give_b(c)
 
     @pl.when(away)
     def _():
         for c in range(PARTS):
-            t_copy(13, c, across).wait_recv()
+            t_copy(2, c, across).wait_recv()
             ring_t.give_a(c)
-            t_copy(15, c, pair).wait_recv()
+            t_copy(3, c, pair).wait_recv()
             ring_t.give_b(c)
 
     for c in range(PARTS):
@@ -496,7 +492,8 @@
     zl = (s // 2) % 4
 
     def hop(c, n, slot, to_slot, to):
-        return remote(kv.at[slot, half(c)], kv.at[to_slot, half(c)], k_send.at[c, n], k_recv.at[c, to_slot], to)
+        r = pl.ds(c * (T // WINS), T // WINS)
+        return remote(kv.at[slot, r], kv.at[to_slot, r], k_send.at[n], k_recv.at[c, to_slot], to)
 
     def own_copy(c, k):
         return hop(c, k, 0, 2 * k, (s + 2 * k, h))
@@ -523,22 +520,24 @@
 
     for c in range(PARTS):
         ring_t.finish(c)
-        for i in range(2):
+        for i in range(HALF // 128):
             r = slice(c * HALF + i * 128, c * HALF + (i + 1) * 128)
             rows_i = tf[r, :].astype(F32)
             mean = jnp.mean(rows_i * rows_i, axis=-1, keepdims=True)
             nrm[r, :] = (rows_i * lax.rsqrt(mean + EPS) * gain[...]).astype(BF16)
         kv[0, half(c), 0:W] = dot(nrm[half(c), :], ak[...]).astype(BF16)
         kv[0, half(c), W : 2 * W] = dot(nrm[half(c), :], av[...]).astype(BF16)
-        for k in (2, 1, 3, 4):
-
-            @pl.when(sends(k))
+        if (c + 1) % (PARTS // WINS) == 0:
+            w = (c + 1) // (PARTS // WINS) - 1
+            for k in (2, 1, 3, 4):
+
+                @pl.when(sends(k))
+                def _():
+                    own_copy(w, k).start()
+
+            @pl.when(par == 0)
             def _():
-                own_copy(c, k).start()
-
-        @pl.when(par == 0)
-        def _():
-            side_copy(c).start()
+                side_copy(w).start()
 
     query = dot(nrm[...], aq[...]).astype(BF16) * 0.125
     low = lax.broadcasted_iota(jnp.int32, (128, W), 1) < 64
@@ -579,7 +578,7 @@
 
         @pl.when((j < 4) & (s >= 2 * k))
         def _():
-            for c in range(PARTS):
+            for c in range(WINS):
                 arrive(c, 2 * k)
 
                 @pl.when((k == 2) & (zl == 2))
@@ -598,7 +597,7 @@
 
         @pl.when((odd > 0) & (odd < 9) & (s >= odd))
         def _():
-            for c in range(PARTS):
+            for c in range(WINS):
                 arrive(c, odd)
             attend(odd, 1)
 
@@ -609,9 +608,12 @@
         both = acc[i, :, 0:W] / acc[i, :, W : 2 * W]
         cf[i * 128 : (i + 1) * 128, col(h)] = jnp.where(low, both[0:128], both[128:256]).astype(BF16)
 
+    def out_copy(c):
+        return pltpu.make_async_copy(ob.at[half(c)], out_ref.at[half(c)], o_sem.at[c])
+
     def c_copy(c):
         ref = cf.at[half(c), col(h)]
-        return send(19 + c, ref, ref, across)
+        return send(5, ref, ref, across, c)
 
     for c in range(PARTS):
         c_copy(c).start()
@@ -619,72 +621,63 @@
     for c in range(PARTS):
         c_copy(c).wait_recv()
         ring_c.give_b(c)
-    for d in range(1, NH):
-        wo_copy(d).wait_recv()
+    wait(wo.at[pl.ds(0, 7 * W)], w_recv)
     for c in range(PARTS):
         ring_c.relay(c)
     for c in range(PARTS):
         ring_c.finish(c)
-        out_ref[half(c), :] = dot(cf[half(c), :], wo[...]).astype(BF16)
+        ob[half(c), :] = dot(cf[half(c), :], wo[...]).astype(BF16)
+        out_copy(c).start()
 
     @pl.when(home)
     def _():
         ring_k.drain()
         ring_q.drain()
-        for c in range(PARTS):
-            side_rows(9, c, kf).wait_send()
-            side_rows(11, c, qf).wait_send()
-            t_copy(13, c, across).wait_send()
+        wait(kf, p_send.at[1])
+        wait(qf, p_send.at[7])
+        wait(tb, p_send.at[2])
         mi_copy().wait_send()
         mo_copy().wait_send()
         w0_copy().wait_send()
 
     @pl.when(away)
     def _():
-        for c in range(PARTS):
-            z_copy(0, c, kb, kf).wait_send()
-            z_copy(2, c, qb, qf).wait_send()
-            t_copy(17, c, aside).wait_send()
-            t_copy(15, c, pair).wait_send()
+        wait(kb, p_send.at[0])
+        wait(qb, p_send.at[6])
+        wait(tb, p_send.at[3])
+        wait(tb, p_send.at[4])
         v_copy().wait_send()
         gate_copy().wait_send()
-        for n in range(2):
-            for d in (1, 2, 3):
-                share_copy(d, n).wait_send()
+        wait(kf.at[pl.ds(0, 192)], x_send)
 
     ring_t.drain()
     ring_c.drain()
-    for c in range(PARTS):
-        c_copy(c).wait_send()
+    wait(kb, p_send.at[5])
+    for c in range(PARTS):
+        out_copy(c).wait()
     for group_copies in (sum_one, sum_two, share_r):
         group_copies.drain()
-    for d in range(1, NH):
-        wo_copy(d).wait_send()
+    wait(wo.at[pl.ds(0, 7 * W)], w_send)
     pltpu.make_async_copy(gates.at[some], gates.at[some], gt_send).wait()
     pltpu.make_async_copy(gbuf.at[some], gbuf.at[some], a_send).wait()
     pltpu.make_async_copy(wbuf.at[some], wbuf.at[some], b_send).wait()
-    for c in range(PARTS):
-        for k in range(1, 5):
-
-            @pl.when(sends(k))
-            def _():
-                own_copy(c, k).wait_send()
-
-            @pl.when(passes(k))
-            def _():
-                pass_copy(c, k).wait_send()
-
-        @pl.when(par == 0)
+    for k in range(1, 5):
+
+        @pl.when(sends(k))
         def _():
-            side_copy(c).wait_send()
-
-        @pl.when((s >= 4) & (zl == 2))
+            wait(kv.at[0], k_send.at[k])
+
+        @pl.when(passes(k))
         def _():
-            relay_copy(c, True).wait_send()
-
-        @pl.when((s >= 4) & (zl == 1))
-        def _():
-            relay_copy(c, False).wait_send()
+            wait(kv.at[0], k_send.at[4 + k])
+
+    @pl.when(par == 0)
+    def _():
+        wait(kv.at[0], k_send.at[0])
+
+    @pl.when((s >= 4) & ((zl == 1) | (zl == 2)))
+    def _():
+        wait(kv.at[0], k_send.at[9])
 
 
 def block(
@@ -703,10 +696,10 @@
         name="titans",
         out_shape=jax.ShapeDtypeStruct((T, W), BF16),
         in_specs=[hb] * 6 + [vm] * 3 + [sm, vm] + [hb] * 4,
-        out_specs=vm,
+        out_specs=hb,
         scratch_shapes=[
             big, V((1024, W), BF16), V((1024, W), BF16), V((1024, W), BF16), V((1024, W), F32), V((W, 1024), F32),
-            V((1024, W), BF16), V((1024, W), BF16), V((1024, W), BF16), V((W, 1024), BF16), dma((10,)),
+            V((1024, W), BF16), V((1024, W), BF16), V((1024, W), BF16), V((W, 1024), BF16), dma((10,)), V((T, W), BF16), dma((PARTS,)),
             big, big, big, big, big,
             V((1024, W), BF16), V((T, W), BF16), V((T, W), BF16), V((T, W), BF16), V((T, W), BF16), V((T, W), BF16),
             V((T, W), BF16), V((T, W), F32), V((T, W), BF16), V((1024, W), BF16), V((W, 1024), BF16), V((1024, W), F32),
@@ -714,9 +707,9 @@
             V((2, 7, T, W), BF16), V((2, 7, T, W), BF16), V((NS, 8, W), F32), V((8, W), F32),
             slab, slab, slab, slab,
             V((9, T, 2 * W), BF16), V((4, 256, W), BF16), big, V((4, 256, 1), F32), V((4, 256, 2 * W), F32),
-            dma((4, PARTS, 6)), dma((4, PARTS, 6)), dma((PARTS, 7)), dma((PARTS, 7)), dma((2, PARTS, 7)), dma((2, PARTS, 7)), dma((21,)), dma((21,)),
-            dma((7,)), dma((7,)), dma, dma,
-            dma, dma((NS,)), dma, dma, dma((PARTS, 10)), dma((PARTS, 9)), dma((2, 3)), dma((2, 3)),
+            dma((4,)), dma((4, PARTS, 3)), dma, dma((PARTS, 4)), dma((2,)), dma((2, PARTS, 4)), dma((13,)), dma((6 * PARTS,)), dma((7,)),
+            dma, dma, dma, dma,
+            dma, dma((NS,)), dma, dma, dma((10,)), dma((WINS, 9)), dma, dma((2,)),
         ],
         compiler_params=pltpu.CompilerParams(collective_id=0, has_side_effects=True, vmem_limit_bytes=60 * 1024 * 1024),
     )(

time: 149 us -> 145 us (0.973)
  Pallas kernels: 146 us -> 142 us
    pallas_call x1, Pallas kernels: 146 us -> 142 us  [block(): pl.pallas_call(kernel, name='titans', out_shape=jax.ShapeDtypeStruct((T,...]
where the time goes in v5:
time: 145 us; the launch traced here: 144 us
  Pallas kernels  142 us (98%)
  local copies, waits for them, and re-layouts  1.57 us (1%)
    pallas_call x1, Pallas kernels, block(): pl.pallas_call(kernel, name='titans', out_shape=jax.ShapeDtypeStruct((T,...  142 us

profile of v5, /device:TPU:6, one launch (start us, length us, event | category | flops | bytes accessed | tf_op | source)
XLA Modules:
  0.0 144.5 jit_solution(1853690475378665370)
XLA Ops:
  0.7 142.3 %titans.1 = bf16[512,128]{1,0:T(8,128)(2,1)} custom-call(bf16[512,1024]{1,0:T(8,128)(2,1)} %tok_h.1, bf16[1024,128]{1,0:T(8,128)(2,1)} %wq_h.1, bf16[1024,128]{1,0:T(8,128)(2,1)} %wk_h.1, bf16[1024,128]{1,0:T(8,128)(2,1)} %wv_h.1, f32[1024,128]{1,0:T(8,128)} %m_in_h.1, f32[128,1024]{1,0:T(8,128)} %m_out_h.1, f32[16,128]{1,0:T(8,128)} %fg.1, f32[16,128]{1,0:T(8,128)} %mo.1, ...), custom_call_target="tpu_custom_call" | custom-call | tf_op jit(solution)/shard_map/titans/pallas_call | solution.py:694
  142.9 1.6 %copy.18 = bf16[512,128]{1,0:T(8,128)(2,1)} copy(bf16[512,128]{1,0:T(8,128)(2,1)} %titans.1) | data formatting | bytes 262144

commit v6 on v5

--- a/solution.py
+++ b/solution.py
@@ -95,14 +95,14 @@
 
 
 class Share:
-    def __init__(self, core, buf, send, recv):
-        self.me, self.buf, self.send, self.recv = core, buf, send, recv
+    def __init__(self, core, ref, four, seven, send, recv):
+        self.me, self.ref, self.four, self.seven, self.send, self.recv = core, ref, four, seven, send, recv
 
     def copy(self, c, n):
         me = self.me
         y = (me.y, me.y, me.prev, me.y, me.prev, me.next, me.far)[n]
         to = (me.at(me.next), me.at(me.prev), me.at(me.next), me.other(), me.other(), me.other(), me.other())[n]
-        ref = self.buf.at[half(c), col(y * 2 + me.k)]
+        ref = self.ref(c, y * 2 + me.k)
         return remote(ref, ref, self.send, self.recv.at[c, min(n, 3)], to)
 
     def start(self, c):
@@ -121,10 +121,10 @@
         self.copy(c, 6).start()
 
     def finish(self, c):
-        wait(self.buf.at[half(c), pl.ds(0, 4 * W)], self.recv.at[c, 3])
+        wait(self.four(c), self.recv.at[c, 3])
 
     def drain(self):
-        wait(self.buf.at[pl.ds(0, T * 7 // 8)], self.send)
+        wait(self.seven, self.send)
 
 
 class Sum:
@@ -177,9 +177,9 @@
 def kernel(
     tok_h, wq_h, wk_h, wv_h, m_in_h, m_out_h, fg, mo, st, plan, gain, aq_h, ak_h, av_h, ao_h, out_ref,
     tok, wk, wq, wv, m_in, m_out, aq, ak, av, ao, l_sem, ob, o_sem,
-    kf, qf, rf, tf, cf, wo, kb, qb, vb, tb, vbuf, hid, slope, hq, mi, mob, mot, w0, w0s, kt,
+    kf, qf, rf, tf, cf, hf, vf, wo, kb, qb, vb, tb, slope, hq, mi, mof, mot, w0, w0s, kt,
     rs_out, rs_land, gates, gown, gbuf, rbuf, wbuf, wland, kv, qs, nrm, m_s, acc,
-    g_send, g_recv, h_send, h_recv, r_send, r_recv, p_send, p_recv, q_recv, w_send, w_recv, gt_send, gt_recv,
+    g_send, g_recv, f_send, f_recv, h_send, h_recv, r_send, r_recv, p_send, p_recv, q_recv, w_send, w_recv, gt_send, gt_recv,
     a_send, a_recv, b_send, b_recv, k_send, k_recv, x_send, x_recv,
 ):
     s, h = lax.axis_index("seq"), lax.axis_index("head")
@@ -244,6 +244,14 @@
     ring_q = Ring(place, z, qf, g_send.at[1], g_recv.at[1])
     ring_t = Ring(place, par, tf, g_send.at[2], g_recv.at[2])
     ring_c = Ring(place, z, cf, g_send.at[3], g_recv.at[3])
+    ring_v = Ring(place, z, vf, g_send.at[4], g_recv.at[4])
+    own = y * 2 + par
+
+    def cols_of(buf):
+        return (lambda c, b: buf.at[half(c), col(b)], lambda c: buf.at[half(c), pl.ds(0, 4 * W)], buf.at[pl.ds(0, T * 7 // 8)])
+
+    share_h = Share(core, *cols_of(hf), h_send, h_recv)
+    share_m = Share(core, lambda c, b: mof.at[col(b)], lambda c: mof.at[pl.ds(0, 4 * W)], mof.at[pl.ds(0, 7 * W)], f_send, f_recv)
 
     x = s // 8
 
@@ -253,25 +261,22 @@
     def side_rows(n, c, buf):
         return send(n, buf.at[half(c)], buf.at[half(c)], aside, c)
 
-    def v_copy():
-        return send(8, vb, vbuf, pair)
-
     def gate_copy():
-        return send(9, gown, gates.at[s], pair)
+        return send(13, gown, gates.at[s], pair)
 
     def mi_copy():
         ref = mi.at[pl.ds(pl.multiple_of(x * 256, 256), 256), :]
         return send(10, ref, ref, across)
 
     def mo_copy():
-        ref = mob.at[pl.ds(pl.multiple_of(x * 32, 32), 32), :]
+        ref = mof.at[pl.ds(pl.multiple_of(own * W + x * 32, 32), 32), :]
         return send(11, ref, ref, across)
 
     def share_copy(d, n):
         if n == 0:
             ref = mi.at[pl.ds(pl.multiple_of(x * 256, 256), 256), :]
         else:
-            ref = mob.at[pl.ds(pl.multiple_of(x * 32, 32), 32), :]
+            ref = mof.at[pl.ds(pl.multiple_of(own * W + x * 32, 32), 32), :]
         return remote(ref, ref, x_send, x_recv.at[n], ((x + d) % 4 * 8 + s % 8, h))
 
     def w0_copy():
@@ -282,7 +287,10 @@
         for c in range(PARTS):
             ring_k.give_a(c)
         mi[...] = m_in[...].astype(BF16)
-        mob[...] = m_out[...].astype(BF16)
+        mof[col(own), :] = m_out[...].astype(BF16)
+        mi_copy().start()
+        mo_copy().start()
+        share_m.start(0)
 
     @pl.when(away)
     def _():
@@ -295,11 +303,9 @@
 
     @pl.when(home)
     def _():
-        mi_copy().start()
-        mo_copy().start()
         mot[...] = m_out[...].T
         qf[:, col(h)] = query
-        vbuf[...] = value
+        vf[:, col(h)] = value
         gates[g] = gown[...]
 
         def rows(c):
@@ -313,8 +319,14 @@
     @pl.when(away)
     def _():
         vb[...] = value
-        v_copy().start()
         gate_copy().start()
+
+    def forward(c):
+        pre = dot(kf[half(c), :], mi[...])
+        sig = jax.nn.sigmoid(pre)
+        hf[half(c), col(own)] = (pre * sig).astype(BF16)
+        slope[half(c), :] = sig * (1.0 + pre * (1.0 - sig))
+        share_h.start(c)
 
     @pl.when(home)
     def _():
@@ -323,9 +335,17 @@
             ring_k.give_b(c)
         for c in range(PARTS):
             ring_k.relay(c)
+        share_m.step(0)
+        for c in range(PARTS):
+            ring_v.give_a(c)
         for c in range(PARTS):
             ring_k.finish(c)
             side_rows(1, c, kf).start()
+            forward(c)
+        wait(vb, q_recv.at[2])
+        for c in range(PARTS):
+            ring_v.give_b(c)
+        share_m.last(0)
 
     @pl.when(away)
     def _():
@@ -333,45 +353,56 @@
             copy().wait_recv()
             for d in (2, 1, 3):
                 share_copy(d, n).start()
+        for c in range(PARTS):
+            z_copy(8, c, vb, vf).start()
+        wait(mof.at[pl.ds(0, 96)], x_recv.at[1])
+        share_m.start(0)
         wait(mi.at[pl.ds(0, 768)], x_recv.at[0])
-        wait(mob.at[pl.ds(0, 96)], x_recv.at[1])
         for c in range(PARTS):
             side_rows(1, c, kf).wait_recv()
+            forward(c)
+        share_m.step(0)
         for c in range(PARTS):
             z_copy(6, c, qb, qf).start()
-
-    pre = dot(kf[...], mi[...])
-    sig = jax.nn.sigmoid(pre)
-    hid[...] = (pre * sig).astype(BF16)
-    slope[...] = sig * (1.0 + pre * (1.0 - sig))
-
-    def part_one(c, b):
-        return dot(hid[half(c), :], mob[:, col(b)])
-
-    sum_one = Sum(core, part_one, rs_out.at[0], rs_land.at[0], r_send.at[0], r_recv.at[0])
-    sum_one.run()
-
-    @pl.when(away)
-    def _():
-        v_copy().wait_recv()
         gate_copy().wait_recv()
         w0_copy().wait_recv()
-
-    own = core.y * 2 + par
-    share_r = Share(core, rf, h_send, h_recv)
-    for c in range(PARTS):
-        rf[half(c), col(own)] = ((2.0 / T) * (sum_one.last(c) - vbuf[half(c), :].astype(F32))).astype(BF16)
-        share_r.start(c)
 
     def send_gates(d, carry):
         remote(gates.at[g], gates.at[g], gt_send, gt_recv, group((g + d) % NS)).start()
         return carry
 
     lax.fori_loop(1, NS, send_gates, 0)
+    for c in range(PARTS):
+        share_h.step(c)
+
+    @pl.when(home)
+    def _():
+        for c in range(PARTS):
+            ring_v.relay(c)
+
+    for c in range(PARTS):
+        share_h.last(c)
+
+    @pl.when(home)
+    def _():
+        for c in range(PARTS):
+            ring_v.finish(c)
+            side_rows(14, c, vf).start()
+
+    @pl.when(away)
+    def _():
+        share_m.last(0)
+
     kt[...] = kf[...].T
-    for stage in (share_r.step, share_r.last, share_r.finish):
-        for c in range(PARTS):
-            stage(c)
+    share_m.finish(0)
+
+    @pl.when(away)
+    def _():
+        wait(vf, q_recv.at[8])
+
+    for c in range(PARTS):
+        share_h.finish(c)
+        rf[half(c), :] = ((2.0 / T) * (dot(hf[half(c), :], mof[...]) - vf[half(c), :].astype(F32))).astype(BF16)
 
     @pl.when(home)
     def _():
@@ -379,9 +410,9 @@
             ring_q.give_a(c)
 
     rate = gates[g][2:3]
-    g_out = dot(hid[...].T, rf[...])
+    g_out = dot(hf[:, col(own)].T, rf[...])
     gbuf[:, 32:64, :] = (g_out.T * -rate).astype(BF16).reshape(NS, 32, W)
-    term = (dot(rf[...], mob[...], NT) * slope[...]).astype(BF16)
+    term = (dot(rf[...], mof[col(own), :], NT) * slope[...]).astype(BF16)
     gbuf[:, 0:32, :] = (dot(kt[...], term) * -rate).astype(BF16).reshape(NS, 32, W)
 
     def send_grad(d, carry):
@@ -452,7 +483,7 @@
     def part_two(c, b):
         return dot(hq[half(c), :], wland[pl.ds(b * 4, 4), 32:64, :].reshape(W, W), NT)
 
-    sum_two = Sum(core, part_two, rs_out.at[1], rs_land.at[1], r_send.at[1], r_recv.at[1])
+    sum_two = Sum(core, part_two, rs_out, rs_land, r_send, r_recv)
     sum_two.run()
 
     def t_copy(n, c, to):
@@ -633,6 +664,8 @@
     def _():
         ring_k.drain()
         ring_q.drain()
+        ring_v.drain()
+        wait(vf, p_send.at[14])
         wait(kf, p_send.at[1])
         wait(qf, p_send.at[7])
         wait(tb, p_send.at[2])
@@ -646,7 +679,7 @@
         wait(qb, p_send.at[6])
         wait(tb, p_send.at[3])
         wait(tb, p_send.at[4])
-        v_copy().wait_send()
+        wait(vb, p_send.at[8])
         gate_copy().wait_send()
         wait(kf.at[pl.ds(0, 192)], x_send)
 
@@ -655,7 +688,7 @@
     wait(kb, p_send.at[5])
     for c in range(PARTS):
         out_copy(c).wait()
-    for group_copies in (sum_one, sum_two, share_r):
+    for group_copies in (sum_two, share_h, share_m):
         group_copies.drain()
     wait(wo.at[pl.ds(0, 7 * W)], w_send)
     pltpu.make_async_copy(gates.at[some], gates.at[some], gt_send).wait()
@@ -700,14 +733,14 @@
         scratch_shapes=[
             big, V((1024, W), BF16), V((1024, W), BF16), V((1024, W), BF16), V((1024, W), F32), V((W, 1024), F32),
             V((1024, W), BF16), V((1024, W), BF16), V((1024, W), BF16), V((W, 1024), BF16), dma((10,)), V((T, W), BF16), dma((PARTS,)),
-            big, big, big, big, big,
-            V((1024, W), BF16), V((T, W), BF16), V((T, W), BF16), V((T, W), BF16), V((T, W), BF16), V((T, W), BF16),
-            V((T, W), BF16), V((T, W), F32), V((T, W), BF16), V((1024, W), BF16), V((W, 1024), BF16), V((1024, W), F32),
+            big, big, big, big, big, big, big,
+            V((1024, W), BF16), V((T, W), BF16), V((T, W), BF16), V((T, W), BF16), V((T, W), BF16),
+            V((T, W), F32), V((T, W), BF16), V((1024, W), BF16), V((1024, 1024), BF16), V((1024, W), F32),
             V((64, W), F32), V((64, W), F32), V((1024, T), BF16),
-            V((2, 7, T, W), BF16), V((2, 7, T, W), BF16), V((NS, 8, W), F32), V((8, W), F32),
+            V((7, T, W), BF16), V((7, T, W), BF16), V((NS, 8, W), F32), V((8, W), F32),
             slab, slab, slab, slab,
             V((9, T, 2 * W), BF16), V((4, 256, W), BF16), big, V((4, 256, 1), F32), V((4, 256, 2 * W), F32),
-            dma((4,)), dma((4, PARTS, 3)), dma, dma((PARTS, 4)), dma((2,)), dma((2, PARTS, 4)), dma((13,)), dma((6 * PARTS,)), dma((7,)),
+            dma((5,)), dma((5, PARTS, 3)), dma, dma((1, 4)), dma, dma((PARTS, 4)), dma, dma((PARTS, 4)), dma((15,)), dma((6 * PARTS,)), dma((9,)),
             dma, dma, dma, dma,
             dma, dma((NS,)), dma, dma, dma((10,)), dma((WINS, 9)), dma, dma((2,)),
         ],

time: 145 us -> 143 us (0.986)
  Pallas kernels: 142 us -> 140 us
    pallas_call x1, Pallas kernels: 142 us -> 140 us  [block(): pl.pallas_call(kernel, name='titans', out_shape=jax.ShapeDtypeStruct((T,...]
where the time goes in v6:
time: 143 us
  Pallas kernels  140 us (98%)
  local copies, waits for them, and re-layouts  1.57 us (1%)
    pallas_call x1, Pallas kernels, block(): pl.pallas_call(kernel, name='titans', out_shape=jax.ShapeDtypeStruct((T,...  140 us

profile of v6, /device:TPU:6, one launch (start us, length us, event | category | flops | bytes accessed | tf_op | source)
XLA Modules:
  0.0 142.7 jit_solution(5668536965177092737)
XLA Ops:
  0.7 140.4 %titans.1 = bf16[512,128]{1,0:T(8,128)(2,1)} custom-call(bf16[512,1024]{1,0:T(8,128)(2,1)} %tok_h.1, bf16[1024,128]{1,0:T(8,128)(2,1)} %wq_h.1, bf16[1024,128]{1,0:T(8,128)(2,1)} %wk_h.1, bf16[1024,128]{1,0:T(8,128)(2,1)} %wv_h.1, f32[1024,128]{1,0:T(8,128)} %m_in_h.1, f32[128,1024]{1,0:T(8,128)} %m_out_h.1, f32[16,128]{1,0:T(8,128)} %fg.1, f32[16,128]{1,0:T(8,128)} %mo.1, ...), custom_call_target="tpu_custom_call" | custom-call | tf_op jit(solution)/shard_map/titans/pallas_call | solution.py:727
  141.1 1.6 %copy.18 = bf16[512,128]{1,0:T(8,128)(2,1)} copy(bf16[512,128]{1,0:T(8,128)(2,1)} %titans.1) | data formatting | bytes 262144

commit v7 on v6

--- a/solution.py
+++ b/solution.py
@@ -560,7 +560,7 @@
         kv[0, half(c), W : 2 * W] = dot(nrm[half(c), :], av[...]).astype(BF16)
         if (c + 1) % (PARTS // WINS) == 0:
             w = (c + 1) // (PARTS // WINS) - 1
-            for k in (2, 1, 3, 4):
+            for k in (2, 4, 3, 1):
 
                 @pl.when(sends(k))
                 def _():

time: 143 us -> 143 us (level)
  no operation moved by 1% of the time
where the time goes in v7:
time: 143 us
  Pallas kernels  140 us (98%)
  local copies, waits for them, and re-layouts  1.57 us (1%)
    pallas_call x1, Pallas kernels, block(): pl.pallas_call(kernel, name='titans', out_shape=jax.ShapeDtypeStruct((T,...  140 us

profile of v7, /device:TPU:6, one launch (start us, length us, event | category | flops | bytes accessed | tf_op | source)
XLA Modules:
  0.0 142.7 jit_solution(1180391019117469883)
XLA Ops:
  0.7 140.4 %titans.1 = bf16[512,128]{1,0:T(8,128)(2,1)} custom-call(bf16[512,1024]{1,0:T(8,128)(2,1)} %tok_h.1, bf16[1024,128]{1,0:T(8,128)(2,1)} %wq_h.1, bf16[1024,128]{1,0:T(8,128)(2,1)} %wk_h.1, bf16[1024,128]{1,0:T(8,128)(2,1)} %wv_h.1, f32[1024,128]{1,0:T(8,128)} %m_in_h.1, f32[128,1024]{1,0:T(8,128)} %m_out_h.1, f32[16,128]{1,0:T(8,128)} %fg.1, f32[16,128]{1,0:T(8,128)} %mo.1, ...), custom_call_target="tpu_custom_call" | custom-call | tf_op jit(solution)/shard_map/titans/pallas_call | solution.py:727
  141.1 1.6 %copy.18 = bf16[512,128]{1,0:T(8,128)(2,1)} copy(bf16[512,128]{1,0:T(8,128)(2,1)} %titans.1) | data formatting | bytes 262144
